TPU v7x, 32 devices: a whole 2x2x4 slice. The times are simulated.
32 devices in a mesh: tp: 8 (over z, y), rep: 4 (over x, core).
Axes of the slice: x: 2, y: 2, z: 4, core: 2. Of those that a mesh axis runs over, the one named last changes fastest.
Arguments:
- tokens: bfloat16 [1536, 8192], P('rep', 'tp'), may hold values from -6 to 6
- row_lengths: int32 [8], P('rep'), may hold values from 1 to 192
- attn_gain: float32 [8192], P('tp'), may hold values from 0.1 to 1.9
- query_weight: bfloat16 [8192, 4096], P('rep', 'tp'), may hold values from -2 to 2
- key_weight: bfloat16 [8192, 512], P('rep', 'tp'), may hold values from -2 to 2
- value_matrix: bfloat16 [8192, 512], P('rep', 'tp'), may hold values from -0.0625 to 0.0625
- output_weight: bfloat16 [4096, 8192], P('rep', 'tp'), may hold values from -0.09375 to 0.09375
- final_gain: float32 [8192], P('tp'), may hold values from 0.1 to 1.9
- value_head: float32 [8192, 6], P('tp'), may hold values from -0.0625 to 0.0625
Outputs:
- resid_out: bfloat16 [1536, 8192], P('rep', 'tp')
- objective_scores: float32 [1536, 6], P('rep')
All inputs are finite; a program needn't handle non-finite values.
Results may differ from a plain program's by a relative error of at most 0.025.
Values may be sent and summed in bfloat16 or wider, within the bound.
A program may use at most 64 MiB of HBM per device.

v0:
```python
import functools
import jax
import jax.numpy as jnp
from jax import lax
from jax.experimental import pallas as pl
from jax.experimental.pallas import tpu as pltpu
from jax.sharding import PartitionSpec as P

KEY_VALUE_HEADS = 4
HEAD_SIZE = 128
EPS = 1e-05
MESH = pl.DeviceIdType.MESH


class Stage:
    def __init__(self, src, dst, buffer, sems):
        self.into = pltpu.make_async_copy(src, buffer, sems.at[0])
        self.out = pltpu.make_async_copy(buffer, dst, sems.at[1])


def slot(ref, dim, size, index, rows=None):
    if rows is not None:
        return ref.at[pl.ds(*rows), pl.ds(pl.multiple_of(index * size, size), size)]
    if dim is None:
        return ref.at[index]
    if isinstance(dim, tuple):
        return ref.at[index, pl.ds(dim[2], dim[1])]
    start = pl.multiple_of(index * size, size)
    return ref.at[pl.ds(start, size)] if dim == 0 else ref.at[:, pl.ds(start, size)]


class Line:
    def __init__(self, axis, count, dim, src, dst, sems, rows=None):
        self.axis, self.dim, self.dst = axis, dim, dst
        self.windowed = isinstance(dim, tuple)
        rows = dim[:2] if self.windowed else rows
        self.src = src if rows is None else src.at[pl.ds(*rows)]
        self.rows = None if self.windowed else rows
        self.count = count
        self.up_sem, self.down_sem, self.pair_sem, self.line_recv, self.pair_recv = sems
        me = lax.axis_index(axis)
        self.me, self.place, self.side = me, me // 2, me % 2
        self.partner = me + 1 - 2 * self.side
        self.size = None if dim is None or self.windowed else src.shape[dim]

    def at(self, index):
        return slot(self.dst, self.dim, self.size, index, self.rows)

    def copy(self, source, index, send, recv, target):
        return pltpu.make_async_remote_copy(
            src_ref=source,
            dst_ref=self.at(index),
            send_sem=send,
            recv_sem=recv,
            device_id={self.axis: target},
            device_id_type=MESH,
        )

    def up(self, source, origin):
        return self.copy(
            source, 2 * origin + self.side, self.up_sem.at[origin], self.line_recv.at[origin], self.me + 2
        )

    def down(self, source, origin):
        return self.copy(
            source, 2 * origin + self.side, self.down_sem.at[origin], self.line_recv.at[origin], self.me - 2
        )

    def pair(self, source, origin):
        return self.copy(
            source,
            2 * origin + self.side,
            self.pair_sem.at[origin],
            self.pair_recv.at[origin],
            self.partner,
        )

    def own_block(self):
        return self.at(self.me)

    def has_up(self):
        return self.place < self.count - 1

    def has_down(self):
        return self.place > 0

    def begin(self):
        @pl.when(self.has_up())
        def _():
            self.up(self.src, self.place).start()

        @pl.when(self.has_down())
        def _():
            self.down(self.src, self.place).start()

        self.pair(self.src, self.place).start()

    def hop(self, step):
        below, above = self.place - step, self.place + step

        @pl.when(below >= 0)
        def _():
            block = self.at(2 * below + self.side)
            self.up(block, below).wait_recv()

            @pl.when(self.has_up())
            def _():
                self.up(block, below).start()

            self.pair(block, below).start()

        @pl.when(above < self.count)
        def _():
            block = self.at(2 * above + self.side)
            self.down(block, above).wait_recv()

            @pl.when(self.has_down())
            def _():
                self.down(block, above).start()

            self.pair(block, above).start()

    def finish(self):
        for origin in range(self.count):
            here = self.at(2 * origin + self.side)
            self.pair(here, origin).wait_send()
            pltpu.make_async_remote_copy(
                src_ref=here,
                dst_ref=self.at(2 * origin + 1 - self.side),
                send_sem=self.pair_sem.at[origin],
                recv_sem=self.pair_recv.at[origin],
                device_id={self.axis: self.partner},
                device_id_type=MESH,
            ).wait_recv()

            @pl.when((origin <= self.place) & self.has_up())
            def _():
                self.up(here, origin).wait_send()

            @pl.when((origin >= self.place) & self.has_down())
            def _():
                self.down(here, origin).wait_send()

    def neighbours(self):
        return ((self.has_up(), self.me + 2), (self.has_down(), self.me - 2), (None, self.partner))


class Cross(Line):
    def __init__(self, axis, count, dim, src, dst, sems, rows):
        super().__init__(axis, count, dim, src, dst, sems, rows)
        self.other = 1 - self.side

    def along(self, source, origin, side, which, step):
        sem = self.up_sem if step > 0 else self.down_sem
        return self.copy(
            source,
            2 * origin + side,
            sem.at[which * self.count + origin],
            self.line_recv.at[which * self.count + origin],
            self.me + step,
        )

    def spread(self, source, origin, which):
        side = self.side if which == 0 else self.other

        @pl.when(self.has_up() & (origin <= self.place))
        def _():
            self.along(source, origin, side, which, 2).start()

        @pl.when(self.has_down() & (origin >= self.place))
        def _():
            self.along(source, origin, side, which, -2).start()

    def across(self, index, source):
        return self.copy(source, index, self.pair_sem.at[0], self.pair_recv.at[0], self.partner)

    def begin(self):
        self.across(self.me, self.src).start()
        self.spread(self.src, self.place, 0)

    def turn(self):
        theirs = self.at(self.partner)
        self.across(self.partner, theirs).wait_recv()
        self.spread(theirs, self.place, 1)

    def hop(self, step):
        for which in range(2):
            side = self.side if which == 0 else self.other
            for origin in (self.place - step, self.place + step):

                @pl.when((origin >= 0) & (origin < self.count))
                def _(origin=origin, side=side, which=which):
                    block = self.at(2 * origin + side)
                    self.along(block, origin, side, which, 2).wait_recv()
                    self.spread(block, origin, which)

    def finish(self):
        self.across(self.me, self.src).wait_send()
        for which in range(2):
            side = self.side if which == 0 else self.other
            for origin in range(self.count):
                block = self.at(2 * origin + side)

                @pl.when((origin <= self.place) & self.has_up())
                def _(origin=origin, side=side, which=which, block=block):
                    self.along(block, origin, side, which, 2).wait_send()

                @pl.when((origin >= self.place) & self.has_down())
                def _(origin=origin, side=side, which=which, block=block):
                    self.along(block, origin, side, which, -2).wait_send()


class Direct:
    def __init__(self, axis, members, src, dst, sems):
        self.axis, self.members, self.src, self.dst = axis, members, src, dst
        self.send, self.recv = sems
        self.me = lax.axis_index(axis)

    def to(self, offset):
        return pltpu.make_async_remote_copy(
            src_ref=self.src,
            dst_ref=self.dst.at[self.me],
            send_sem=self.send.at[offset - 1],
            recv_sem=self.recv.at[offset - 1],
            device_id={self.axis: lax.rem(self.me + offset, self.members)},
            device_id_type=MESH,
        )

    def come(self, offset):
        return pltpu.make_async_remote_copy(
            src_ref=self.src,
            dst_ref=self.dst.at[lax.rem(self.me - offset + self.members, self.members)],
            send_sem=self.send.at[offset - 1],
            recv_sem=self.recv.at[offset - 1],
            device_id={self.axis: lax.rem(self.me + offset, self.members)},
            device_id_type=MESH,
        )

    def own_block(self):
        return self.dst.at[self.me]

    def begin(self):
        for offset in range(1, self.members):
            self.to(offset).start()

    def finish(self):
        for offset in range(1, self.members):
            self.to(offset).wait_send()
            self.come(offset).wait_recv()


def gather_kernel(plan, sizes, *refs):
    count = len(plan)
    sources, targets = refs[:count], refs[count : 2 * count]
    rest = list(refs[2 * count :])

    def take(number):
        taken = rest[:number]
        del rest[:number]
        return taken

    jobs, stages = [], []
    for (kind, axis, dim), src, dst in zip(plan, sources, targets):
        if kind == "fill":
            dst = targets[dim]
            buffer, sems = take(2)
            stages.append(Stage(src, dst.at[:, pl.ds(axis, src.shape[1])], buffer, sems))
            continue
        if kind == "direct":
            made = [Direct(axis, sizes[axis], src, dst, take(2))]
        elif kind == "line":
            made = [Line(axis, sizes[axis] // 2, dim, src, dst, take(5))]
        else:
            first, second = cut(src.shape[0])
            made = [
                Line(axis, sizes[axis] // 2, dim, src, dst, take(5), first),
                Cross(axis, sizes[axis] // 2, dim, src, dst, take(5), second),
            ]
        for job in made:
            buffer, sems = take(2)
            stages.append(Stage(job.src, job.own_block(), buffer, sems))
        jobs += made
    barrier = pltpu.get_barrier_semaphore()
    direct_axes = {job.axis for job in jobs if isinstance(job, Direct)}
    greeted, peers = set(), 0
    for job in jobs:
        if job.axis in greeted:
            continue
        greeted.add(job.axis)
        if job.axis in direct_axes:
            members = sizes[job.axis]
            peers = peers + members - 1
            for offset in range(1, members):
                pl.semaphore_signal(
                    barrier,
                    inc=1,
                    device_id={job.axis: lax.rem(job.me + offset, members)},
                    device_id_type=MESH,
                )
        else:
            for there, target in job.neighbours():
                def signal(target=target, job=job):
                    pl.semaphore_signal(
                        barrier, inc=1, device_id={job.axis: target}, device_id_type=MESH
                    )

                if there is None:
                    peers = peers + 1
                    signal()
                else:
                    peers = peers + there.astype(jnp.int32)
                    pl.when(there)(signal)
    pl.semaphore_wait(barrier, peers)
    for job in jobs:
        job.begin()
    for stage in stages:
        stage.into.start()
    for stage in stages:
        stage.into.wait()
        stage.out.start()
    for job in jobs:
        if isinstance(job, Cross):
            job.turn()
    for axis in ("tp", "rep"):
        lines = [job for job in jobs if isinstance(job, Line) and job.axis == axis]
        for step in range(1, max([job.count for job in lines], default=1)):
            for job in lines:
                job.hop(step)
    for job in jobs:
        job.finish()
    for stage in stages:
        stage.out.wait()


def cut(total):
    cross = total // (6 * 16) * 16
    return (0, total - cross), (total - cross, cross)


def gather(plan, sizes, arrays, collective_id, memory=pl.ANY):
    shapes, scratch = [], []
    dma = pltpu.SemaphoreType.DMA
    for (kind, axis, dim), array in zip(plan, arrays):
        if kind == "fill":
            shapes.append(jax.ShapeDtypeStruct((8, 128), array.dtype))
            scratch += [pltpu.VMEM(array.shape, array.dtype), dma((2,))]
            continue
        members = sizes[axis]
        if dim is None:
            shape = (members,) + array.shape
        elif isinstance(dim, tuple):
            shape = (members, dim[2] + dim[1]) + array.shape[1:]
        else:
            shape = tuple(n * members if i == dim else n for i, n in enumerate(array.shape))
        shapes.append(jax.ShapeDtypeStruct(shape, array.dtype))
        whole = pltpu.VMEM(array.shape, array.dtype)
        if kind == "direct":
            scratch += [dma((members - 1,))] * 2 + [whole, dma((2,))]
        elif kind == "line":
            if isinstance(dim, tuple):
                whole = pltpu.VMEM(dim[1:2] + array.shape[1:], array.dtype)
            scratch += [dma((members // 2,))] * 5 + [whole, dma((2,))]
        else:
            scratch += [dma((members // 2,))] * 5 + [dma((members,))] * 5
            for _, length in cut(array.shape[0]):
                scratch += [pltpu.VMEM((length,) + array.shape[1:], array.dtype), dma((2,))]
    return pl.pallas_call(
        functools.partial(gather_kernel, plan, sizes),
        out_shape=tuple(shapes),
        in_specs=[pl.BlockSpec(memory_space=memory)] * len(arrays),
        out_specs=tuple([pl.BlockSpec(memory_space=memory)] * len(arrays)),
        scratch_shapes=scratch,
        compiler_params=pltpu.CompilerParams(collective_id=collective_id, has_side_effects=True),
    )(*arrays)


def local(
    sizes,
    tokens,
    row_lengths,
    attn_gain,
    query_weight,
    key_weight,
    value_matrix,
    output_weight,
    final_gain,
    value_head,
):
    width = tokens.shape[1] * sizes["tp"]
    rows_here = tokens.shape[0]
    head_cols = query_weight.shape[1]
    kv_cols = key_weight.shape[1]
    xfloat = tokens.astype(jnp.float32)
    squares_here = jnp.sum(xfloat * xfloat, axis=1)[None, :]
    gained = (xfloat * attn_gain).astype(jnp.bfloat16)
    packed = jnp.concatenate([query_weight, key_weight, value_matrix], axis=1)
    first = output_weight.shape[0] // 16
    early = output_weight.shape[0] // 4
    columns, weights, out_first, squares_all = gather(
        (
            ("split", "tp", 1),
            ("line", "rep", 0),
            ("line", "rep", (0, first, 0)),
            ("direct", "tp", None),
        ),
        sizes,
        (gained, packed, output_weight, squares_here),
        0,
    )
    first_scale = lax.rsqrt(jnp.sum(squares_all, axis=(0, 1)) / width + EPS)[:, None]
    projected = jnp.dot(columns, weights, preferred_element_type=jnp.float32)
    projected = (projected * first_scale).astype(jnp.bfloat16)
    query = projected[:, :head_cols]
    kv_all, out_early = gather(
        (("line", "tp", None), ("line", "rep", (first, early, 0))),
        sizes,
        (projected[:, head_cols:], output_weight),
        1,
    )
    sequence_rows = row_lengths.shape[0]
    length = rows_here // sequence_rows
    local_heads = head_cols // HEAD_SIZE
    key_full = kv_all[:, :, :kv_cols].transpose(1, 0, 2).reshape(rows_here, -1)
    value_full = kv_all[:, :, kv_cols:].transpose(1, 0, 2).reshape(rows_here, -1)
    first_head = lax.axis_index("tp") * local_heads
    key_value_index = (first_head + jnp.arange(local_heads, dtype=jnp.int32)) % KEY_VALUE_HEADS
    query4 = query.reshape(sequence_rows, length, local_heads, HEAD_SIZE)
    key4 = key_full.reshape(sequence_rows, length, KEY_VALUE_HEADS, HEAD_SIZE)
    value4 = value_full.reshape(sequence_rows, length, KEY_VALUE_HEADS, HEAD_SIZE)
    if local_heads % KEY_VALUE_HEADS or local_heads != KEY_VALUE_HEADS:
        key4 = jnp.take(key4, key_value_index, axis=2)
        value4 = jnp.take(value4, key_value_index, axis=2)
    scores = jnp.einsum(
        "rqhd,rkhd->rhqk", query4, key4, preferred_element_type=jnp.float32
    ) * (1.0 / HEAD_SIZE**0.5)
    position = jnp.arange(length, dtype=jnp.int32)
    causal = position[None, :] <= position[:, None]
    allowed = causal[None, None, :, :] & (
        position[None, None, None, :] < row_lengths[:, None, None, None]
    )
    scores = jnp.where(allowed, scores, jnp.float32(-1e30))
    scores = scores - jnp.max(scores, axis=3, keepdims=True)
    expo = jnp.exp(scores)
    probs = (expo / jnp.sum(expo, axis=3, keepdims=True)).astype(jnp.bfloat16)
    attended = jnp.einsum(
        "rhqk,rkhd->rqhd", probs, value4, preferred_element_type=jnp.float32
    )
    attended = attended.astype(jnp.bfloat16).reshape(rows_here, head_cols)
    before = first + early
    late = (before, output_weight.shape[0] - before, before)
    mixed, out_weights, _, _ = gather(
        (("split", "tp", 1), ("line", "rep", late), ("fill", 0, 1), ("fill", first, 1)),
        sizes,
        (attended, output_weight, out_first, out_early),
        2,
    )
    out_weights = out_weights.reshape(-1, tokens.shape[1])
    update = jnp.dot(mixed, out_weights, preferred_element_type=jnp.float32)
    resid_out = (xfloat + update).astype(jnp.bfloat16)
    rfloat = resid_out.astype(jnp.float32)
    squares = jnp.sum(rfloat * rfloat, axis=1)
    local_scores = jnp.dot(rfloat * final_gain, value_head, precision=lax.Precision.HIGHEST)
    stats = jnp.concatenate([local_scores.T, squares[None, :]], axis=0)
    (stats_all,) = gather((("direct", "tp", None),), sizes, (stats,), 3)
    stats = jnp.sum(stats_all, axis=0)
    logits = (stats[:-1] * lax.rsqrt(stats[-1:] / width + EPS)).T
    live = (position[None, :] < row_lengths[:, None]).reshape(rows_here, 1)
    objective_scores = jnp.where(live, logits, jnp.float32(0.0))
    return (resid_out, objective_scores)


def solution(mesh):
    in_specs = (
        P("rep", "tp"),
        P("rep"),
        P("tp"),
        P("rep", "tp"),
        P("rep", "tp"),
        P("rep", "tp"),
        P("rep", "tp"),
        P("tp"),
        P("tp", None),
    )
    out_specs = (P("rep", "tp"), P("rep", None))
    body = functools.partial(local, dict(mesh.shape))
    return jax.shard_map(body, mesh=mesh, in_specs=in_specs, out_specs=out_specs, check_vma=False)
```

profile of v0, /device:TPU:0, one launch (start us, length us, event | category | flops | bytes accessed | tf_op | source)
XLA Modules:
  0.0 177.2 jit_solution(16792197451573032325)
XLA Ops:
  0.7 2.4 %fusion.5 = (f32[384]{0:T(512)S(1)}, bf16[384,1024]{1,0:T(8,128)(2,1)}) fusion(bf16[384,1024]{1,0:T(8,128)(2,1)} %param.9, f32[1024]{0:T(1024)} %param.11), kind=kLoop, calls=%fused_computation.11 | loop fusion | flops 1965696 | bytes 1578496 | tf_op jit(solution)/shard_map/reduce_sum | solution.py:394
  3.1 0.6 broadcast_in_dim.24.refs_3_
  3.6 1.2 copy.16
  5.2 1.9 %pad_maximum_fusion.refs_1_ = bf16[2048,640]{1,0:T(8,128)(2,1)} fusion(bf16[2048,64]{1,0:T(8,128)(2,1)S(1)} %copy.17, bf16[2048,64]{1,0:T(8,128)(2,1)S(1)} %copy.16, bf16[2048,512]{1,0:T(8,128)(2,1)S(1)} %copy-done.1), kind=kLoop, calls=%fused_computation.1 | loop fusion | flops 7864320 | bytes 5242880 | tf_op jit(solution)/shard_map/concatenate | solution.py:396
  7.0 77.5 %shard_map.104 = (bf16[384,8192]{1,0:T(8,128)(2,1)}, bf16[8192,640]{1,0:T(8,128)(2,1)}, bf16[4,64,1024]{2,1,0:T(8,128)(2,1)}, f32[8,1,384]{2,1,0:T(1,128)}) custom-call(bf16[384,1024]{1,0:T(8,128)(2,1)} %get-tuple-element.21.refs_0_, bf16[2048,640]{1,0:T(8,128)(2,1)} %pad_maximum_fusion.refs_1_, bf16[1024,1024]{1,0:T(8,128)(2,1)} %refs_1_.3, ...), custom_call_target="tpu_custom_call" | custom-call | tf_op jit(solution)/shard_map/pallas_call | solution.py:367
  84.5 0.7 reduce_sum.46
  85.3 10.2 %fusion.8 = bf16[384,640]{1,0:T(8,128)(2,1)S(1)} fusion(bf16[384,8192]{1,0:T(8,128)(2,1)} %get-tuple-element.10, bf16[8192,640]{1,0:T(8,128)(2,1)} %get-tuple-element.11, f32[384]{0:T(512)S(1)} %add_rsqrt_fusion), kind=kOutput, calls=%fused_computation.17 | convolution fusion | flops 4027023360 | bytes 17270272 | tf_op jit(solution)/shard_map/dot_general | solution.py:411
  95.5 0.6 slice.24.refs_0_
  96.1 16.8 %shard_map.105 = (bf16[8,384,128]{2,1,0:T(8,128)(2,1)}, bf16[4,256,1024]{2,1,0:T(8,128)(2,1)}) custom-call(bf16[384,128]{1,0:T(8,128)(2,1)} %slice.24.refs_0_, bf16[1024,1024]{1,0:T(8,128)(2,1)} %refs_1_.3), custom_call_target="tpu_custom_call" | custom-call | tf_op jit(solution)/shard_map/pallas_call | solution.py:367
  112.9 1.7 slice_bitcast_fusion.1
  114.6 0.3 copy.19
  114.9 0.3 reshape_reshape.7
  115.6 0.8 fusion.31
  116.4 0.3 copy.18
  117.0 0.5 fusion.9
  117.5 0.3 copy.24
  117.8 0.8 copy.46
  118.6 40.1 %shard_map.106 = (bf16[384,4096]{1,0:T(8,128)(2,1)}, bf16[4,1024,1024]{2,1,0:T(8,128)(2,1)}, bf16[8,128]{1,0:T(8,128)(2,1)}, bf16[8,128]{1,0:T(8,128)(2,1)}) custom-call(bf16[384,512]{1,0:T(8,128)(2,1)} %bitcast.25, bf16[1024,1024]{1,0:T(8,128)(2,1)} %refs_1_.3, bf16[4,64,1024]{2,1,0:T(8,128)(2,1)} %get-tuple-element.14.refs_2_, ...), custom_call_target="tpu_custom_call" | custom-call | tf_op jit(solution)/shard_map/pallas_call | solution.py:367
  158.7 7.9 %fusion.3 = (f32[384]{0:T(512)S(1)}, bf16[384,1024]{1,0:T(8,128)(2,1)S(1)}) fusion(bf16[384,4096]{1,0:T(8,128)(2,1)} %get-tuple-element.16, bf16[4096,1024]{1,0:T(8,128)(2,1)} %bitcast.27, bf16[384,1024]{1,0:T(8,128)(2,1)S(1)} %copy-done.2), kind=kOutput, calls=%fused_computation.9 | convolution fusion | flops 3223584256 | bytes 13108736 | tf_op jit(solution)/shard_map/dot_general | solution.py:458
  166.6 1.5 fusion.10
  168.1 0.6 pad_maximum_fusion.1.refs_0_
  168.7 6.9 %shard_map.107 = f32[8,7,384]{2,1,0:T(8,128)} custom-call(f32[7,384]{1,0:T(8,128)} %pad_maximum_fusion.1.refs_0_), custom_call_target="tpu_custom_call" | custom-call | tf_op jit(solution)/shard_map/pallas_call | solution.py:367
  175.6 0.9 reduce_sum.49
  176.6 0.6 fusion.20
  (25 shorter events, 1.1 us)
Async XLA Ops:
  0.6 166.0 %copy-start = (f32[1024,6]{0,1:T(8,128)S(1)}, f32[1024,6]{0,1:T(8,128)}, u32[]{:S(2)}) copy-start(f32[1024,6]{0,1:T(8,128)} %param.17) | copy-start | bytes 73732
  0.6 4.2 %copy-start.4 = (bf16[2048,64]{0,1:T(8,128)(2,1)S(1)}, bf16[2048,64]{0,1:T(8,128)(2,1)}, u32[]{:S(2)}) copy-start(bf16[2048,64]{0,1:T(8,128)(2,1)} %param.14) | copy-start | bytes 786436
  0.7 4.5 %copy-start.1 = (bf16[2048,512]{1,0:T(8,128)(2,1)S(1)}, bf16[2048,512]{1,0:T(8,128)(2,1)}, u32[]{:S(2)}) copy-start(bf16[2048,512]{1,0:T(8,128)(2,1)} %param.12) | copy-start | bytes 6291460
  114.6 0.8 copy-start.6
  118.6 40.1 %copy-start.2 = (bf16[384,1024]{1,0:T(8,128)(2,1)S(1)}, bf16[384,1024]{1,0:T(8,128)(2,1)}, u32[]{:S(2)}) copy-start(bf16[384,1024]{1,0:T(8,128)(2,1)} %param.9) | copy-start | bytes 2359300
  158.7 7.9 %copy-start.5 = (f32[1024]{0:T(1024)S(1)}, f32[1024]{0:T(1024)}, u32[]{:S(2)}) copy-start(f32[1024]{0:T(1024)} %param.16) | copy-start | bytes 12292
  166.6 10.6 %copy-start.3 = (bf16[384,1024]{1,0:T(8,128)(2,1)}, bf16[384,1024]{1,0:T(8,128)(2,1)S(1)}, u32[]{:S(2)}) copy-start(bf16[384,1024]{1,0:T(8,128)(2,1)S(1)} %get-tuple-element.25) | copy-start | bytes 2359300
where the time goes:
time: 178 us; the launch traced here: 177 us
  Pallas kernels  141 us (79%)
  matrix products  20.8 us (12%)
  other arithmetic  7.4 us (4%)
  local copies, waits for them, and re-layouts  6.93 us (4%)
    pallas_call x4, Pallas kernels, gather(): pl.pallas_call(functools.partial(gather_kernel, plan, sizes), out_shape=t...  141 us
    dot_general x1, matrix products, local(): projected = jnp.dot(columns, weights, preferred_element_type=jnp.float32)  10.2 us
    dot_general x1, matrix products, local(): update = jnp.dot(mixed, out_weights, preferred_element_type=jnp.float32)  7.88 us

commit v1 on v0

--- a/solution.py
+++ b/solution.py
@@ -10,6 +10,8 @@
 HEAD_SIZE = 128
 EPS = 1e-05
 MESH = pl.DeviceIdType.MESH
+STEP = 256
+SEMAPHORES = 512
 
 
 class Stage:
@@ -469,6 +471,577 @@
     return (resid_out, objective_scores)
 
 
+class Pool:
+    def __init__(self, ref):
+        self.ref, self.used = ref, 0
+
+    def take(self, number):
+        base = self.used
+        self.used += number
+        return lambda index: self.ref.at[base + index]
+
+
+class Route:
+    def __init__(self, axis, size, view, pool):
+        self.axis, self.view, self.count = axis, view, size // 2
+        self.me = lax.axis_index(axis)
+        self.place, self.side = self.me // 2, self.me % 2
+        self.partner = self.me + 1 - 2 * self.side
+        self.has_up = self.place < self.count - 1
+        self.has_down = self.place > 0
+        self.pool = pool
+        self.make(pool)
+
+    def copy(self, index, send, recv, target):
+        return pltpu.make_async_remote_copy(
+            src_ref=self.view(index),
+            dst_ref=self.view(index),
+            send_sem=send,
+            recv_sem=recv,
+            device_id={self.axis: target},
+            device_id_type=MESH,
+        )
+
+
+class Row(Route):
+    def make(self, pool):
+        n = self.count
+        self.up_sem, self.down_sem, self.pair_sem = pool.take(n), pool.take(n), pool.take(n)
+        self.line_recv, self.pair_recv = pool.take(n), pool.take(n)
+
+    def up(self, origin):
+        index = 2 * origin + self.side
+        return self.copy(index, self.up_sem(origin), self.line_recv(origin), self.me + 2)
+
+    def down(self, origin):
+        index = 2 * origin + self.side
+        return self.copy(index, self.down_sem(origin), self.line_recv(origin), self.me - 2)
+
+    def pair(self, origin, side):
+        index = 2 * origin + side
+        return self.copy(index, self.pair_sem(origin), self.pair_recv(origin), self.partner)
+
+    def begin(self):
+        pl.when(self.has_up)(lambda: self.up(self.place).start())
+        pl.when(self.has_down)(lambda: self.down(self.place).start())
+        self.pair(self.place, self.side).start()
+
+    def hop(self, step):
+        below, above = self.place - step, self.place + step
+
+        @pl.when(below >= 0)
+        def _():
+            self.up(below).wait_recv()
+            pl.when(self.has_up)(lambda: self.up(below).start())
+            self.pair(below, self.side).start()
+
+        @pl.when(above < self.count)
+        def _():
+            self.down(above).wait_recv()
+            pl.when(self.has_down)(lambda: self.down(above).start())
+            self.pair(above, self.side).start()
+
+    def gathered(self):
+        for origin in range(self.count):
+            self.pair(origin, 1 - self.side).wait_recv()
+
+    def drain(self):
+        for origin in range(self.count):
+            self.pair(origin, self.side).wait_send()
+            pl.when((origin <= self.place) & self.has_up)(lambda: self.up(origin).wait_send())
+            pl.when((origin >= self.place) & self.has_down)(lambda: self.down(origin).wait_send())
+
+
+class Crossed(Route):
+    def make(self, pool):
+        n = 2 * self.count
+        self.up_sem, self.down_sem, self.line_recv = pool.take(n), pool.take(n), pool.take(n)
+        self.pair_sem, self.pair_recv = pool.take(1), pool.take(1)
+        self.sides = (self.side, 1 - self.side)
+
+    def along(self, origin, which, step):
+        number = which * self.count + origin
+        sem = (self.up_sem if step > 0 else self.down_sem)(number)
+        index = 2 * origin + self.sides[which]
+        return self.copy(index, sem, self.line_recv(number), self.me + step)
+
+    def spread(self, origin, which):
+        up, down = self.has_up & (origin <= self.place), self.has_down & (origin >= self.place)
+        pl.when(up)(lambda: self.along(origin, which, 2).start())
+        pl.when(down)(lambda: self.along(origin, which, -2).start())
+
+    def across(self, index):
+        return self.copy(index, self.pair_sem(0), self.pair_recv(0), self.partner)
+
+    def begin(self):
+        self.across(self.me).start()
+        self.spread(self.place, 0)
+
+    def turn(self):
+        self.across(self.partner).wait_recv()
+        self.spread(self.place, 1)
+
+    def hop(self, step):
+        for which in range(2):
+            for origin in (self.place - step, self.place + step):
+
+                @pl.when((origin >= 0) & (origin < self.count))
+                def _(origin=origin, which=which):
+                    self.along(origin, which, 2).wait_recv()
+                    self.spread(origin, which)
+
+    def gathered(self):
+        pass
+
+    def drain(self):
+        self.across(self.me).wait_send()
+        for which in range(2):
+            for origin in range(self.count):
+                up = (origin <= self.place) & self.has_up
+                down = (origin >= self.place) & self.has_down
+                pl.when(up)(lambda: self.along(origin, which, 2).wait_send())
+                pl.when(down)(lambda: self.along(origin, which, -2).wait_send())
+
+
+class Both:
+    def __init__(self, *parts):
+        self.parts = parts
+
+    def begin(self):
+        for part in self.parts:
+            part.begin()
+
+    def turn(self):
+        for part in self.parts:
+            if isinstance(part, Crossed):
+                part.turn()
+
+    def hop(self, step):
+        for part in self.parts:
+            part.hop(step)
+
+    def gathered(self):
+        for part in self.parts:
+            part.gathered()
+
+    def drain(self):
+        for part in self.parts:
+            part.drain()
+
+
+class Everyone:
+    def __init__(self, axis, size, view, pool):
+        self.axis, self.size, self.view = axis, size, view
+        self.me = lax.axis_index(axis)
+        self.send, self.recv = pool.take(size - 1), pool.take(size - 1)
+
+    def copy(self, index, offset):
+        return pltpu.make_async_remote_copy(
+            src_ref=self.view(index),
+            dst_ref=self.view(index),
+            send_sem=self.send(offset - 1),
+            recv_sem=self.recv(offset - 1),
+            device_id={self.axis: lax.rem(self.me + offset, self.size)},
+            device_id_type=MESH,
+        )
+
+    def begin(self):
+        for offset in range(1, self.size):
+            self.copy(self.me, offset).start()
+
+    def gathered(self):
+        for offset in range(1, self.size):
+            self.copy(lax.rem(self.me - offset + self.size, self.size), offset).wait_recv()
+
+    def drain(self):
+        for offset in range(1, self.size):
+            self.copy(self.me, offset).wait_send()
+
+
+NT = (((1,), (1,)), ((), ()))
+
+
+def dot(a, b):
+    return jnp.dot(a, b, preferred_element_type=jnp.float32)
+
+
+def dot_nt(a, b):
+    return lax.dot_general(a, b, NT, preferred_element_type=jnp.float32)
+
+
+def exact_parts(values, number):
+    parts = []
+    for _ in range(number):
+        part = values.astype(jnp.bfloat16)
+        parts.append(part)
+        values = values - part.astype(jnp.float32)
+    return parts
+
+
+def row_sums_of_squares(block):
+    wide = block.astype(jnp.float32)
+    ones = jnp.ones((16, block.shape[1]), jnp.bfloat16)
+    high, low = exact_parts(wide * wide, 2)
+    return (dot_nt(ones, high) + dot_nt(ones, low))[:8]
+
+
+def layer_kernel(
+    sizes,
+    lengths_s,
+    tokens_h,
+    gain_h,
+    query_h,
+    key_h,
+    value_h,
+    output_h,
+    final_h,
+    head_h,
+    resid_h,
+    score_h,
+    tok_all,
+    wkv_all,
+    wq_all,
+    wo_all,
+    kv_all,
+    att_all,
+    sq_all,
+    stat_all,
+    raw,
+    gain,
+    fgain,
+    heads,
+    qbuf,
+    resid,
+    score,
+    dma,
+    local_dma,
+):
+    tp, rep = sizes["tp"], sizes["rep"]
+    me_t, me_r = lax.axis_index("tp"), lax.axis_index("rep")
+    pool, here = Pool(dma), Pool(local_dma)
+    width = tp * tokens_h.shape[1]
+    features = tokens_h.shape[1]
+    sequences = lengths_s.shape[0]
+    length = tokens_h.shape[0] // sequences
+    kv_cols = key_h.shape[0]
+    per_rep = tp // rep
+    q_steps, q_cols = wq_all.shape[0], wq_all.shape[3]
+    o_steps, o_cols = wo_all.shape[0], wo_all.shape[3]
+    head_cols = q_steps * q_cols
+    per_head = HEAD_SIZE // kv_cols
+    crossing = length // (6 * 16) * 16
+
+    def fetch(src, dst):
+        made = pltpu.make_async_copy(src, dst, here.take(1)(0))
+        made.start()
+        return made
+
+    def rows_of(s):
+        return pl.ds(s * length, length)
+
+    def gather_rows(buffer, s):
+        start = s * length
+        straight = pl.ds(start, length - crossing)
+        rest = pl.ds(start + length - crossing, crossing)
+        return Both(
+            Crossed("tp", tp, lambda i: buffer.at[i, rest], pool),
+            Row("tp", tp, lambda i: buffer.at[i, straight], pool),
+        )
+
+    token_jobs = [gather_rows(tok_all, s) for s in range(sequences)]
+    att_jobs = [gather_rows(att_all, s) for s in range(sequences)]
+    kv_jobs = [Row("tp", tp, lambda i, s=s: kv_all.at[s, i], pool) for s in range(sequences)]
+    wkv_job = Row("rep", rep, lambda i: wkv_all.at[i], pool)
+    wq_jobs = [Row("rep", rep, lambda i, j=j: wq_all.at[j, i], pool) for j in range(q_steps)]
+    wo_jobs = [Row("rep", rep, lambda i, n=n: wo_all.at[n, i], pool) for n in range(o_steps)]
+    sq_job = Everyone("tp", tp, lambda i: sq_all.at[i], pool)
+    stat_jobs = [Everyone("tp", tp, lambda i, s=s: stat_all.at[s, i], pool) for s in range(sequences)]
+
+    load_tokens = fetch(tokens_h, raw)
+    load_gain = fetch(gain_h, gain)
+    load_kv = [
+        fetch(key_h, wkv_all.at[me_r, pl.ds(0, kv_cols)]),
+        fetch(value_h, wkv_all.at[me_r, pl.ds(kv_cols, kv_cols)]),
+    ]
+    load_q = [
+        fetch(query_h.at[:, pl.ds(j * q_cols, q_cols)], wq_all.at[j, me_r]) for j in range(q_steps)
+    ]
+    load_o = [
+        fetch(output_h.at[:, pl.ds(n * o_cols, o_cols)], wo_all.at[n, me_r]) for n in range(o_steps)
+    ]
+    load_final = [fetch(final_h, fgain), fetch(head_h, heads)]
+
+    barrier = pltpu.get_barrier_semaphore()
+    for axis, me, size in (("tp", me_t, tp), ("rep", me_r, rep)):
+        for offset in range(1, size):
+            pl.semaphore_signal(
+                barrier,
+                inc=1,
+                device_id={axis: lax.rem(me + offset, size)},
+                device_id_type=MESH,
+            )
+
+    load_tokens.wait()
+    load_gain.wait()
+    for s in range(sequences):
+        block = raw[rows_of(s), :].astype(jnp.float32) * gain[...]
+        tok_all[me_t, rows_of(s), :] = block.astype(jnp.bfloat16)
+    for copy in load_kv:
+        copy.wait()
+    pl.semaphore_wait(barrier, tp + rep - 2)
+
+    token_jobs[0].begin()
+    wkv_job.begin()
+    for copy, job in zip(load_q, wq_jobs):
+        copy.wait()
+        job.begin()
+    for copy, job in zip(load_o, wo_jobs):
+        copy.wait()
+        job.begin()
+    sq_all[me_t] = row_sums_of_squares(raw[...])
+    token_jobs[0].turn()
+    sq_job.begin()
+    for copy in load_final:
+        copy.wait()
+    token_jobs[0].hop(1)
+    for job in token_jobs[1:]:
+        job.begin()
+        job.turn()
+    wkv_job.hop(1)
+    for step in range(2, rep // 2):
+        wkv_job.hop(step)
+
+    def row_scale(s):
+        total = sq_all[0, :, rows_of(s)]
+        for t in range(1, tp):
+            total = total + sq_all[t, :, rows_of(s)]
+        return lax.rsqrt(total / width + EPS)
+
+    def project_kv(s):
+        total = jnp.zeros((2 * kv_cols, length), jnp.float32)
+        for t in range(tp):
+            weight = wkv_all[t // per_rep, :, pl.ds(t % per_rep * features, features)]
+            total = total + dot_nt(weight, tok_all[t, rows_of(s), :])
+        kv_all[s, me_t] = (total * row_scale(s)[:1]).astype(jnp.bfloat16)
+        kv_jobs[s].begin()
+
+    def project_q(s, j):
+        total = jnp.zeros((length, q_cols), jnp.float32)
+        for t in range(tp):
+            weight = wq_all[j, t // per_rep, pl.ds(t % per_rep * features, features), :]
+            total = total + dot(tok_all[t, rows_of(s), :], weight)
+        column = row_scale(s).T[:, :1]
+        qbuf[s, :, pl.ds(j * q_cols, q_cols)] = (total * column).astype(jnp.bfloat16)
+
+    def attend(s):
+        here_length = lengths_s[s]
+        query_at = lax.broadcasted_iota(jnp.int32, (length, length), 0)
+        key_at = lax.broadcasted_iota(jnp.int32, (length, length), 1)
+        allowed = (key_at <= query_at) & (key_at < here_length)
+        for h in range(head_cols // HEAD_SIZE):
+            first = h % KEY_VALUE_HEADS * per_head
+            blocks = [kv_all[s, first + b] for b in range(per_head)]
+            keys = jnp.concatenate([b[:kv_cols] for b in blocks], axis=0)
+            values = jnp.concatenate([b[kv_cols:] for b in blocks], axis=0)
+            query = qbuf[s, :, pl.ds(h * HEAD_SIZE, HEAD_SIZE)]
+            scores = dot(query, keys) * (1.0 / HEAD_SIZE**0.5)
+            scores = jnp.where(allowed, scores, jnp.float32(-1e30))
+            expo = jnp.exp(scores - jnp.max(scores, axis=1, keepdims=True))
+            probs = (expo / jnp.sum(expo, axis=1, keepdims=True)).astype(jnp.bfloat16)
+            mixed = dot_nt(probs, values).astype(jnp.bfloat16)
+            att_all[me_t, rows_of(s), pl.ds(h * HEAD_SIZE, HEAD_SIZE)] = mixed
+        att_jobs[s].begin()
+
+    def project_out(s, n):
+        cols = pl.ds(n * o_cols, o_cols)
+        total = raw[rows_of(s), cols].astype(jnp.float32)
+        update = jnp.zeros((length, o_cols), jnp.float32)
+        for t in range(tp):
+            weight = wo_all[n, t // per_rep, pl.ds(t % per_rep * head_cols, head_cols), :]
+            update = update + dot(att_all[t, rows_of(s), :], weight)
+        resid[rows_of(s), cols] = (total + update).astype(jnp.bfloat16)
+
+    def statistics(s):
+        block = resid[rows_of(s), :]
+        weight = heads[...] * fgain[...]
+        weight = jnp.concatenate([weight, jnp.zeros((8 - heads.shape[0], features), jnp.float32)], axis=0)
+        parts = [p.astype(jnp.float32) for p in exact_parts(weight, 3)]
+        stacked = jnp.concatenate(parts + [jnp.zeros_like(weight)], axis=0).astype(jnp.bfloat16)
+        sums = dot_nt(stacked, block)
+        sums = sums[0:8] + sums[8:16] + sums[16:24]
+        squares = row_sums_of_squares(block)
+        line = lax.broadcasted_iota(jnp.int32, sums.shape, 0)
+        stat_all[s, me_t] = jnp.where(line == 7, squares, sums)
+        stat_jobs[s].begin()
+
+    def conclude(s):
+        stat_jobs[s].gathered()
+        total = stat_all[s, 0]
+        for t in range(1, tp):
+            total = total + stat_all[s, t]
+        score[s] = total * lax.rsqrt(total[7:8] / width + EPS)
+
+    def write_out(s):
+        return fetch(resid.at[rows_of(s)], resid_h.at[rows_of(s)])
+
+    token_jobs[0].hop(2)
+    token_jobs[1].hop(1)
+    for step in range(3, tp // 2):
+        token_jobs[0].hop(step)
+        token_jobs[1].hop(step - 1)
+    wq_jobs[0].hop(1)
+    token_jobs[0].gathered()
+    sq_job.gathered()
+    wkv_job.gathered()
+    project_kv(0)
+    token_jobs[1].hop(tp // 2 - 1)
+    wq_jobs[0].gathered()
+    project_q(0, 0)
+    for step in range(1, tp // 2):
+        kv_jobs[0].hop(step)
+    for j in range(1, q_steps):
+        wq_jobs[j].hop(1)
+        wq_jobs[j].gathered()
+        project_q(0, j)
+    kv_jobs[0].gathered()
+    attend(0)
+    token_jobs[1].gathered()
+    project_kv(1)
+    att_jobs[0].turn()
+    kv_jobs[1].hop(1)
+    project_q(1, 0)
+    att_jobs[0].hop(1)
+    kv_jobs[1].hop(2)
+    for j in range(1, q_steps):
+        project_q(1, j)
+    for step in range(3, tp // 2):
+        kv_jobs[1].hop(step)
+    kv_jobs[1].gathered()
+    attend(1)
+    wo_jobs[0].hop(1)
+    att_jobs[1].turn()
+    att_jobs[0].hop(2)
+    wo_jobs[1].hop(1)
+    att_jobs[1].hop(1)
+    for step in range(3, tp // 2):
+        att_jobs[0].hop(step)
+        att_jobs[1].hop(step - 1)
+    att_jobs[0].gathered()
+    for n in range(2):
+        wo_jobs[n].gathered()
+        project_out(0, n)
+    att_jobs[1].hop(tp // 2 - 1)
+    for n in range(2, o_steps):
+        wo_jobs[n].hop(1)
+        wo_jobs[n].gathered()
+        project_out(0, n)
+    statistics(0)
+    writes = [write_out(0)]
+    att_jobs[1].gathered()
+    for n in range(o_steps):
+        project_out(1, n)
+    statistics(1)
+    writes.append(write_out(1))
+    conclude(0)
+    conclude(1)
+    last = fetch(score, score_h)
+    for job in token_jobs + att_jobs + kv_jobs + [wkv_job] + wq_jobs + wo_jobs + [sq_job] + stat_jobs:
+        job.drain()
+    for copy in writes:
+        copy.wait()
+    last.wait()
+
+
+def whole_layer(
+    sizes,
+    tokens,
+    row_lengths,
+    attn_gain,
+    query_weight,
+    key_weight,
+    value_matrix,
+    output_weight,
+    final_gain,
+    value_head,
+):
+    tp, rep = sizes["tp"], sizes["rep"]
+    rows, features = tokens.shape
+    sequences = row_lengths.shape[0]
+    length = rows // sequences
+    depth, head_cols = query_weight.shape
+    kv_cols = key_weight.shape[1]
+    mixed = output_weight.shape[0]
+    vmem, dma = pltpu.VMEM, pltpu.SemaphoreType.DMA
+    half, single = jnp.bfloat16, jnp.float32
+    q_steps, o_steps = head_cols // STEP, features // STEP
+    anywhere = pl.BlockSpec(memory_space=pl.ANY)
+    resid, score = pl.pallas_call(
+        functools.partial(layer_kernel, sizes),
+        out_shape=(
+            jax.ShapeDtypeStruct((rows, features), half),
+            jax.ShapeDtypeStruct((sequences, 8, length), single),
+        ),
+        in_specs=[pl.BlockSpec(memory_space=pltpu.SMEM)] + [anywhere] * 8,
+        out_specs=(anywhere, anywhere),
+        scratch_shapes=[
+            vmem((tp, rows, features), half),
+            vmem((rep, 2 * kv_cols, depth), half),
+            vmem((q_steps, rep, depth, STEP), half),
+            vmem((o_steps, rep, mixed, STEP), half),
+            vmem((sequences, tp, 2 * kv_cols, length), half),
+            vmem((tp, rows, head_cols), half),
+            vmem((tp, 8, rows), single),
+            vmem((sequences, tp, 8, length), single),
+            vmem((rows, features), half),
+            vmem((1, features), single),
+            vmem((1, features), single),
+            vmem((value_head.shape[1], features), single),
+            vmem((sequences, length, head_cols), half),
+            vmem((rows, features), half),
+            vmem((sequences, 8, length), single),
+            dma((SEMAPHORES,)),
+            dma((32,)),
+        ],
+        compiler_params=pltpu.CompilerParams(
+            collective_id=4, has_side_effects=True, vmem_limit_bytes=64 * 1024 * 1024 - 128 * 1024
+        ),
+    )(
+        row_lengths,
+        tokens,
+        attn_gain[None, :],
+        query_weight,
+        key_weight.T,
+        value_matrix.T,
+        output_weight,
+        final_gain[None, :],
+        value_head.T,
+    )
+    position = jnp.arange(length, dtype=jnp.int32)
+    live = position[None, :] < row_lengths[:, None]
+    score = jnp.where(live[:, None, :], score[:, : value_head.shape[1]], jnp.float32(0.0))
+    return resid, score.transpose(0, 2, 1).reshape(rows, -1)
+
+
+def fits(sizes, tokens, row_lengths, query_weight, key_weight):
+    heads = query_weight.shape[1] // HEAD_SIZE
+    return (
+        row_lengths.shape[0] == 2
+        and sizes["rep"] == 4
+        and sizes["tp"] % sizes["rep"] == 0
+        and sizes["tp"] >= 8
+        and heads > 0
+        and heads % KEY_VALUE_HEADS == 0
+        and query_weight.shape[1] % STEP == 0
+        and tokens.shape[1] % STEP == 0
+        and HEAD_SIZE % key_weight.shape[1] == 0
+    )
+
+
+def layer(sizes, tokens, row_lengths, attn_gain, query_weight, key_weight, *rest):
+    chosen = whole_layer if fits(sizes, tokens, row_lengths, query_weight, key_weight) else local
+    return chosen(sizes, tokens, row_lengths, attn_gain, query_weight, key_weight, *rest)
+
+
 def solution(mesh):
     in_specs = (
         P("rep", "tp"),
@@ -482,5 +1055,5 @@
         P("tp", None),
     )
     out_specs = (P("rep", "tp"), P("rep", None))
-    body = functools.partial(local, dict(mesh.shape))
+    body = functools.partial(layer, dict(mesh.shape))
     return jax.shard_map(body, mesh=mesh, in_specs=in_specs, out_specs=out_specs, check_vma=False)

time: 178 us -> 139 us (0.78)
  matrix products: 20.8 us -> 0 us
  other arithmetic: 7.4 us -> 0.79 us
  Pallas kernels: 141 us -> 135 us
  local copies, waits for them, and re-layouts: 6.93 us -> 2.76 us
    dot_general x4 -> x0, matrix products: 20.1 us -> none  [the longest x1 10.2 us: local(): projected = jnp.dot(columns, weights, preferred_element_type=jnp.float32)]
    pallas_call x4 -> x1, Pallas kernels: 141 us -> 135 us  [whole_layer(): pl.pallas_call(functools.partial(layer_kernel, sizes), out_shape=(jax.Sha...]
    reduce_sum x3 -> x0, other arithmetic: 4.04 us -> none  [the longest x1 2.39 us: local(): squares_here = jnp.sum(xfloat * xfloat, axis=1)[None, :]]
    concatenate x2 -> x0, other arithmetic: 2.51 us -> none  [the longest x1 1.89 us: local(): packed = jnp.concatenate([query_weight, key_weight, value_matrix], axis=1)]
    transpose x3 -> x1, local copies, waits for them, and re-layouts: 2.3 us -> 0.01 us  [whole_layer(): return (resid, score.transpose(0, 2, 1).reshape(rows, -1))]
where the time goes in v1:
time: 139 us
  Pallas kernels  135 us (97%)
  local copies, waits for them, and re-layouts  2.76 us (2%)
    pallas_call x1, Pallas kernels, whole_layer(): pl.pallas_call(functools.partial(layer_kernel, sizes), out_shape=(jax.Sha...  135 us

profile of v1, /device:TPU:0, one launch (start us, length us, event | category | flops | bytes accessed | tf_op | source)
XLA Modules:
  0.0 139.1 jit_solution(2710638086019312021)
XLA Ops:
  0.6 0.0 copy-start
  0.6 134.9 %shard_map.104 = (bf16[384,1024]{1,0:T(8,128)(2,1)}, f32[2,8,192]{2,1,0:T(8,128)}) custom-call(s32[2]{0:T(128)} %lengths_s.1, bf16[384,1024]{1,0:T(8,128)(2,1)} %tokens_h.1, f32[1,1024]{1,0:T(1,128)} %bitcast.12, bf16[2048,512]{1,0:T(8,128)(2,1)} %query_h.1, bf16[64,2048]{1,0:T(8,128)(2,1)} %bitcast.9, bf16[64,2048]{1,0:T(8,128)(2,1)} %bitcast.10, ...), custom_call_target="tpu_custom_call" | custom-call | tf_op jit(solution)/shard_map/pallas_call | solution.py:978
  135.5 0.0 copy-done
  135.5 0.1 iota_compare_fusion
  135.6 0.7 select_bitcast_fusion
  136.3 0.7 reshape.24
  137.0 2.1 %copy.13 = bf16[384,1024]{1,0:T(8,128)(2,1)} copy(bf16[384,1024]{1,0:T(8,128)(2,1)} %get-tuple-element.8) | data formatting | bytes 1572864
  (1 shorter events, 0.0 us)
Async XLA Ops:
  0.6 134.9 %copy-start = (s32[2]{0:T(128)S(1)}, s32[2]{0:T(128)}, u32[]{:S(2)}) copy-start(s32[2]{0:T(128)} %lengths_s.1) | copy-start | bytes 28

commit v2 on v1

--- a/solution.py
+++ b/solution.py
@@ -11,7 +11,7 @@
 EPS = 1e-05
 MESH = pl.DeviceIdType.MESH
 STEP = 256
-SEMAPHORES = 512
+SEMAPHORES = 126
 
 
 class Stage:
@@ -471,6 +471,9 @@
     return (resid_out, objective_scores)
 
 
+UP, DOWN = True, False
+
+
 class Pool:
     def __init__(self, ref):
         self.ref, self.used = ref, 0
@@ -482,180 +485,166 @@
 
 
 class Route:
-    def __init__(self, axis, size, view, pool):
-        self.axis, self.view, self.count = axis, view, size // 2
+    def __init__(self, axis, size, span, pool):
+        self.axis, self.span, self.size, self.count = axis, span, size, size // 2
         self.me = lax.axis_index(axis)
         self.place, self.side = self.me // 2, self.me % 2
         self.partner = self.me + 1 - 2 * self.side
         self.has_up = self.place < self.count - 1
         self.has_down = self.place > 0
-        self.pool = pool
+        self.ready = False
         self.make(pool)
 
-    def copy(self, index, send, recv, target):
+    def need(self):
+        if not self.ready:
+            self.ready = True
+            self.gathered()
+
+    def arrive(self):
+        self.hop(1, UP)
+        self.hop(1, DOWN)
+
+    def copy(self, first, number, send, recv, target):
         return pltpu.make_async_remote_copy(
-            src_ref=self.view(index),
-            dst_ref=self.view(index),
+            src_ref=self.span(first, number),
+            dst_ref=self.span(first, number),
             send_sem=send,
             recv_sem=recv,
             device_id={self.axis: target},
             device_id_type=MESH,
         )
 
+    def sent(self, sem, number_at):
+        numbers = [number_at(place) for place in range(self.count)]
+        for number in sorted(set(numbers) - {0}):
+            here = self.place < 0
+            for place, other in enumerate(numbers):
+                if other == number:
+                    here = here | (self.place == place)
+            pl.when(here)(lambda: self.copy(0, number, sem, sem, self.partner).wait_send())
+
+    def ups(self, place):
+        return place + 1 if place < self.count - 1 else 0
+
+    def downs(self, place):
+        return self.count - place if place > 0 else 0
+
 
 class Row(Route):
     def make(self, pool):
-        n = self.count
-        self.up_sem, self.down_sem, self.pair_sem = pool.take(n), pool.take(n), pool.take(n)
-        self.line_recv, self.pair_recv = pool.take(n), pool.take(n)
+        self.line_sem, self.pair_sem, self.pair_recv = pool.take(1)(0), pool.take(1)(0), pool.take(1)(0)
+        self.line_recv = pool.take(self.count - 1)
 
     def up(self, origin):
         index = 2 * origin + self.side
-        return self.copy(index, self.up_sem(origin), self.line_recv(origin), self.me + 2)
+        return self.copy(index, 1, self.line_sem, self.line_recv(origin), self.me + 2)
 
     def down(self, origin):
         index = 2 * origin + self.side
-        return self.copy(index, self.down_sem(origin), self.line_recv(origin), self.me - 2)
-
-    def pair(self, origin, side):
-        index = 2 * origin + side
-        return self.copy(index, self.pair_sem(origin), self.pair_recv(origin), self.partner)
+        return self.copy(index, 1, self.line_sem, self.line_recv(origin - 1), self.me - 2)
+
+    def pair(self, origin):
+        index = 2 * origin + self.side
+        return self.copy(index, 1, self.pair_sem, self.pair_recv, self.partner)
 
     def begin(self):
         pl.when(self.has_up)(lambda: self.up(self.place).start())
         pl.when(self.has_down)(lambda: self.down(self.place).start())
-        self.pair(self.place, self.side).start()
-
-    def hop(self, step):
-        below, above = self.place - step, self.place + step
-
-        @pl.when(below >= 0)
+        self.pair(self.place).start()
+
+    def hop(self, step, upward):
+        origin = self.place - step if upward else self.place + step
+
+        @pl.when((origin >= 0) & (origin < self.count))
         def _():
-            self.up(below).wait_recv()
-            pl.when(self.has_up)(lambda: self.up(below).start())
-            self.pair(below, self.side).start()
-
-        @pl.when(above < self.count)
-        def _():
-            self.down(above).wait_recv()
-            pl.when(self.has_down)(lambda: self.down(above).start())
-            self.pair(above, self.side).start()
+            if upward:
+                self.up(origin).wait_recv()
+                pl.when(self.has_up)(lambda: self.up(origin).start())
+            else:
+                self.down(origin).wait_recv()
+                pl.when(self.has_down)(lambda: self.down(origin).start())
+            self.pair(origin).start()
 
     def gathered(self):
-        for origin in range(self.count):
-            self.pair(origin, 1 - self.side).wait_recv()
+        self.copy(0, self.count, self.pair_sem, self.pair_recv, self.partner).wait_recv()
 
     def drain(self):
-        for origin in range(self.count):
-            self.pair(origin, self.side).wait_send()
-            pl.when((origin <= self.place) & self.has_up)(lambda: self.up(origin).wait_send())
-            pl.when((origin >= self.place) & self.has_down)(lambda: self.down(origin).wait_send())
+        self.copy(0, self.count, self.pair_sem, self.pair_recv, self.partner).wait_send()
+        self.sent(self.line_sem, lambda place: self.ups(place) + self.downs(place))
 
 
 class Crossed(Route):
     def make(self, pool):
-        n = 2 * self.count
-        self.up_sem, self.down_sem, self.line_recv = pool.take(n), pool.take(n), pool.take(n)
-        self.pair_sem, self.pair_recv = pool.take(1), pool.take(1)
-        self.sides = (self.side, 1 - self.side)
-
-    def along(self, origin, which, step):
-        number = which * self.count + origin
-        sem = (self.up_sem if step > 0 else self.down_sem)(number)
-        index = 2 * origin + self.sides[which]
-        return self.copy(index, sem, self.line_recv(number), self.me + step)
-
-    def spread(self, origin, which):
-        up, down = self.has_up & (origin <= self.place), self.has_down & (origin >= self.place)
-        pl.when(up)(lambda: self.along(origin, which, 2).start())
-        pl.when(down)(lambda: self.along(origin, which, -2).start())
+        self.up_sem, self.down_sem = pool.take(1)(0), pool.take(1)(0)
+        self.pair_sem, self.pair_recv = pool.take(1)(0), pool.take(1)(0)
+        self.line_recv = pool.take(self.count - 1)
+
+    def up(self, origin):
+        return self.copy(2 * origin, 2, self.up_sem, self.line_recv(origin), self.me + 2)
+
+    def down(self, origin):
+        return self.copy(2 * origin, 2, self.down_sem, self.line_recv(origin - 1), self.me - 2)
 
     def across(self, index):
-        return self.copy(index, self.pair_sem(0), self.pair_recv(0), self.partner)
+        return self.copy(index, 1, self.pair_sem, self.pair_recv, self.partner)
 
     def begin(self):
         self.across(self.me).start()
-        self.spread(self.place, 0)
 
     def turn(self):
         self.across(self.partner).wait_recv()
-        self.spread(self.place, 1)
-
-    def hop(self, step):
-        for which in range(2):
-            for origin in (self.place - step, self.place + step):
-
-                @pl.when((origin >= 0) & (origin < self.count))
-                def _(origin=origin, which=which):
-                    self.along(origin, which, 2).wait_recv()
-                    self.spread(origin, which)
+        pl.when(self.has_up)(lambda: self.up(self.place).start())
+        pl.when(self.has_down)(lambda: self.down(self.place).start())
+
+    def hop(self, step, upward):
+        origin = self.place - step if upward else self.place + step
+
+        @pl.when((origin >= 0) & (origin < self.count))
+        def _():
+            if upward:
+                self.up(origin).wait_recv()
+                pl.when(self.has_up)(lambda: self.up(origin).start())
+            else:
+                self.down(origin).wait_recv()
+                pl.when(self.has_down)(lambda: self.down(origin).start())
 
     def gathered(self):
         pass
 
     def drain(self):
         self.across(self.me).wait_send()
-        for which in range(2):
-            for origin in range(self.count):
-                up = (origin <= self.place) & self.has_up
-                down = (origin >= self.place) & self.has_down
-                pl.when(up)(lambda: self.along(origin, which, 2).wait_send())
-                pl.when(down)(lambda: self.along(origin, which, -2).wait_send())
-
-
-class Both:
-    def __init__(self, *parts):
-        self.parts = parts
-
-    def begin(self):
-        for part in self.parts:
-            part.begin()
-
-    def turn(self):
-        for part in self.parts:
-            if isinstance(part, Crossed):
-                part.turn()
-
-    def hop(self, step):
-        for part in self.parts:
-            part.hop(step)
-
-    def gathered(self):
-        for part in self.parts:
-            part.gathered()
-
-    def drain(self):
-        for part in self.parts:
-            part.drain()
+        self.sent(self.up_sem, lambda place: 2 * self.ups(place))
+        self.sent(self.down_sem, lambda place: 2 * self.downs(place))
 
 
 class Everyone:
-    def __init__(self, axis, size, view, pool):
-        self.axis, self.size, self.view = axis, size, view
+    def __init__(self, axis, size, span, pool):
+        self.axis, self.size, self.span = axis, size, span
         self.me = lax.axis_index(axis)
-        self.send, self.recv = pool.take(size - 1), pool.take(size - 1)
-
-    def copy(self, index, offset):
+        self.send, self.recv = pool.take(1)(0), pool.take(1)(0)
+
+    def copy(self, first, number, target):
         return pltpu.make_async_remote_copy(
-            src_ref=self.view(index),
-            dst_ref=self.view(index),
-            send_sem=self.send(offset - 1),
-            recv_sem=self.recv(offset - 1),
-            device_id={self.axis: lax.rem(self.me + offset, self.size)},
+            src_ref=self.span(first, number),
+            dst_ref=self.span(first, number),
+            send_sem=self.send,
+            recv_sem=self.recv,
+            device_id={self.axis: target},
             device_id_type=MESH,
         )
 
     def begin(self):
         for offset in range(1, self.size):
-            self.copy(self.me, offset).start()
+            self.copy(self.me, 1, lax.rem(self.me + offset, self.size)).start()
+
+    def all(self):
+        return self.copy(0, self.size - 1, lax.rem(self.me + 1, self.size))
 
     def gathered(self):
-        for offset in range(1, self.size):
-            self.copy(lax.rem(self.me - offset + self.size, self.size), offset).wait_recv()
+        self.all().wait_recv()
 
     def drain(self):
-        for offset in range(1, self.size):
-            self.copy(self.me, offset).wait_send()
+        self.all().wait_send()
 
 
 NT = (((1,), (1,)), ((), ()))
@@ -710,6 +699,7 @@
     gain,
     fgain,
     heads,
+    judge,
     qbuf,
     resid,
     score,
@@ -743,26 +733,48 @@
         start = s * length
         straight = pl.ds(start, length - crossing)
         rest = pl.ds(start + length - crossing, crossing)
-        return Both(
-            Crossed("tp", tp, lambda i: buffer.at[i, rest], pool),
-            Row("tp", tp, lambda i: buffer.at[i, straight], pool),
-        )
-
-    token_jobs = [gather_rows(tok_all, s) for s in range(sequences)]
-    att_jobs = [gather_rows(att_all, s) for s in range(sequences)]
-    kv_jobs = [Row("tp", tp, lambda i, s=s: kv_all.at[s, i], pool) for s in range(sequences)]
-    wkv_job = Row("rep", rep, lambda i: wkv_all.at[i], pool)
-    wq_jobs = [Row("rep", rep, lambda i, j=j: wq_all.at[j, i], pool) for j in range(q_steps)]
-    wo_jobs = [Row("rep", rep, lambda i, n=n: wo_all.at[n, i], pool) for n in range(o_steps)]
-    sq_job = Everyone("tp", tp, lambda i: sq_all.at[i], pool)
-    stat_jobs = [Everyone("tp", tp, lambda i, s=s: stat_all.at[s, i], pool) for s in range(sequences)]
-
-    load_tokens = fetch(tokens_h, raw)
-    load_gain = fetch(gain_h, gain)
+        return [
+            Crossed("tp", tp, lambda i, n: buffer(pl.ds(i, n), rest), pool),
+            Row("tp", tp, lambda i, n: buffer(pl.ds(i, n), straight), pool),
+        ]
+
+    tok = [gather_rows(lambda i, r: tok_all.at[i, r], s) for s in range(sequences)]
+    att = [
+        [gather_rows(lambda i, r, j=j: att_all.at[j, i, r], s) for j in range(q_steps)]
+        for s in range(sequences)
+    ]
+    kv = [Row("tp", tp, lambda i, n, s=s: kv_all.at[s, pl.ds(i, n)], pool) for s in range(sequences)]
+    stat = Everyone("tp", tp, lambda i, n: stat_all.at[pl.ds(i, n)], pool)
+    sq = Row("tp", tp, lambda i, n: sq_all.at[pl.ds(i, n)], pool)
+    wkv = Row("rep", rep, lambda i, n: wkv_all.at[pl.ds(i, n)], pool)
+    wq = [
+        Row("rep", rep, lambda i, m, j=j: wq_all.at[j, pl.ds(i, m)], pool) for j in range(q_steps)
+    ]
+    wo = [
+        Row("rep", rep, lambda i, m, n=n: wo_all.at[n, pl.ds(i, m)], pool) for n in range(o_steps)
+    ]
+    assert pool.used <= SEMAPHORES
+    barrier = pltpu.get_barrier_semaphore()
+    expected = 0
+    for route in (sq, wkv):
+        for there, target in (
+            (route.has_up, route.me + 2),
+            (route.has_down, route.me - 2),
+            (route.place >= 0, route.partner),
+        ):
+            expected = expected + there.astype(jnp.int32)
+
+            @pl.when(there)
+            def _(axis=route.axis, target=target):
+                pl.semaphore_signal(
+                    barrier, inc=1, device_id={axis: target}, device_id_type=MESH
+                )
+
     load_kv = [
         fetch(key_h, wkv_all.at[me_r, pl.ds(0, kv_cols)]),
         fetch(value_h, wkv_all.at[me_r, pl.ds(kv_cols, kv_cols)]),
     ]
+    load_tokens = [fetch(gain_h, gain), fetch(tokens_h, raw)]
     load_q = [
         fetch(query_h.at[:, pl.ds(j * q_cols, q_cols)], wq_all.at[j, me_r]) for j in range(q_steps)
     ]
@@ -771,45 +783,25 @@
     ]
     load_final = [fetch(final_h, fgain), fetch(head_h, heads)]
 
-    barrier = pltpu.get_barrier_semaphore()
-    for axis, me, size in (("tp", me_t, tp), ("rep", me_r, rep)):
-        for offset in range(1, size):
-            pl.semaphore_signal(
-                barrier,
-                inc=1,
-                device_id={axis: lax.rem(me + offset, size)},
-                device_id_type=MESH,
-            )
-
-    load_tokens.wait()
-    load_gain.wait()
+    for copy in load_kv + load_tokens:
+        copy.wait()
     for s in range(sequences):
         block = raw[rows_of(s), :].astype(jnp.float32) * gain[...]
         tok_all[me_t, rows_of(s), :] = block.astype(jnp.bfloat16)
-    for copy in load_kv:
-        copy.wait()
-    pl.semaphore_wait(barrier, tp + rep - 2)
-
-    token_jobs[0].begin()
-    wkv_job.begin()
-    for copy, job in zip(load_q, wq_jobs):
+    pl.semaphore_wait(barrier, expected)
+    wkv.begin()
+    for copy, job in zip(load_q, wq):
         copy.wait()
         job.begin()
-    for copy, job in zip(load_o, wo_jobs):
+    tok[0][0].begin()
+    sq_all[me_t] = row_sums_of_squares(raw[...])
+    sq.begin()
+    tok[0][1].begin()
+    for copy, job in zip(load_o, wo):
         copy.wait()
         job.begin()
-    sq_all[me_t] = row_sums_of_squares(raw[...])
-    token_jobs[0].turn()
-    sq_job.begin()
     for copy in load_final:
         copy.wait()
-    token_jobs[0].hop(1)
-    for job in token_jobs[1:]:
-        job.begin()
-        job.turn()
-    wkv_job.hop(1)
-    for step in range(2, rep // 2):
-        wkv_job.hop(step)
 
     def row_scale(s):
         total = sq_all[0, :, rows_of(s)]
@@ -818,14 +810,17 @@
         return lax.rsqrt(total / width + EPS)
 
     def project_kv(s):
+        for job in tok[s] + [wkv, sq]:
+            job.need()
         total = jnp.zeros((2 * kv_cols, length), jnp.float32)
         for t in range(tp):
             weight = wkv_all[t // per_rep, :, pl.ds(t % per_rep * features, features)]
             total = total + dot_nt(weight, tok_all[t, rows_of(s), :])
         kv_all[s, me_t] = (total * row_scale(s)[:1]).astype(jnp.bfloat16)
-        kv_jobs[s].begin()
+        kv[s].begin()
 
     def project_q(s, j):
+        wq[j].need()
         total = jnp.zeros((length, q_cols), jnp.float32)
         for t in range(tp):
             weight = wq_all[j, t // per_rep, pl.ds(t % per_rep * features, features), :]
@@ -833,12 +828,14 @@
         column = row_scale(s).T[:, :1]
         qbuf[s, :, pl.ds(j * q_cols, q_cols)] = (total * column).astype(jnp.bfloat16)
 
-    def attend(s):
+    def attend(s, j):
+        kv[s].need()
         here_length = lengths_s[s]
         query_at = lax.broadcasted_iota(jnp.int32, (length, length), 0)
         key_at = lax.broadcasted_iota(jnp.int32, (length, length), 1)
         allowed = (key_at <= query_at) & (key_at < here_length)
-        for h in range(head_cols // HEAD_SIZE):
+        for i in range(q_cols // HEAD_SIZE):
+            h = j * (q_cols // HEAD_SIZE) + i
             first = h % KEY_VALUE_HEADS * per_head
             blocks = [kv_all[s, first + b] for b in range(per_head)]
             keys = jnp.concatenate([b[:kv_cols] for b in blocks], axis=0)
@@ -849,107 +846,219 @@
             expo = jnp.exp(scores - jnp.max(scores, axis=1, keepdims=True))
             probs = (expo / jnp.sum(expo, axis=1, keepdims=True)).astype(jnp.bfloat16)
             mixed = dot_nt(probs, values).astype(jnp.bfloat16)
-            att_all[me_t, rows_of(s), pl.ds(h * HEAD_SIZE, HEAD_SIZE)] = mixed
-        att_jobs[s].begin()
-
-    def project_out(s, n):
-        cols = pl.ds(n * o_cols, o_cols)
-        total = raw[rows_of(s), cols].astype(jnp.float32)
+            att_all[j, me_t, rows_of(s), pl.ds(i * HEAD_SIZE, HEAD_SIZE)] = mixed
+        for job in att[s][j]:
+            job.begin()
+
+    def out_block(s, n):
+        rows = pl.ds(pl.multiple_of(s * length, length), length)
+        cols = pl.ds(pl.multiple_of(n * o_cols, o_cols), o_cols)
         update = jnp.zeros((length, o_cols), jnp.float32)
         for t in range(tp):
-            weight = wo_all[n, t // per_rep, pl.ds(t % per_rep * head_cols, head_cols), :]
-            update = update + dot(att_all[t, rows_of(s), :], weight)
-        resid[rows_of(s), cols] = (total + update).astype(jnp.bfloat16)
-
-    def statistics(s):
-        block = resid[rows_of(s), :]
+            for j in range(q_steps):
+                weight = wo_all[n, t // per_rep, pl.ds(t % per_rep * head_cols + j * q_cols, q_cols), :]
+                update = update + dot(att_all[j, t, rows, :], weight)
+        block = (raw[rows, cols].astype(jnp.float32) + update).astype(jnp.bfloat16)
+        resid[rows, cols] = block
+        sums = dot_nt(judge[:, cols], block)
+        sums = sums[0:8] + sums[8:16] + sums[16:24]
+        line = lax.broadcasted_iota(jnp.int32, sums.shape, 0)
+        sums = jnp.where(line == 7, row_sums_of_squares(block), sums)
+        stat_all[me_t, s] += sums
+        return 0
+
+    def project_out(s):
+        for job in sum(att[s], wo[:-1]):
+            job.need()
+        lax.fori_loop(0, o_steps - 1, lambda n, _: out_block(s, n), 0)
+
+    def project_last():
+        wo[-1].need()
+        lax.fori_loop(0, sequences, lambda s, _: out_block(s, o_steps - 1), 0)
+
+    def judges():
         weight = heads[...] * fgain[...]
-        weight = jnp.concatenate([weight, jnp.zeros((8 - heads.shape[0], features), jnp.float32)], axis=0)
+        rest = jnp.zeros((8 - heads.shape[0], features), jnp.float32)
+        weight = jnp.concatenate([weight, rest], axis=0)
         parts = [p.astype(jnp.float32) for p in exact_parts(weight, 3)]
-        stacked = jnp.concatenate(parts + [jnp.zeros_like(weight)], axis=0).astype(jnp.bfloat16)
-        sums = dot_nt(stacked, block)
-        sums = sums[0:8] + sums[8:16] + sums[16:24]
-        squares = row_sums_of_squares(block)
-        line = lax.broadcasted_iota(jnp.int32, sums.shape, 0)
-        stat_all[s, me_t] = jnp.where(line == 7, squares, sums)
-        stat_jobs[s].begin()
+        stat_all[me_t] = jnp.zeros(stat_all.shape[1:], jnp.float32)
+        judge[...] = jnp.concatenate(parts + [jnp.zeros_like(weight)], axis=0).astype(jnp.bfloat16)
 
     def conclude(s):
-        stat_jobs[s].gathered()
-        total = stat_all[s, 0]
+        total = stat_all[0, s]
         for t in range(1, tp):
-            total = total + stat_all[s, t]
-        score[s] = total * lax.rsqrt(total[7:8] / width + EPS)
-
-    def write_out(s):
-        return fetch(resid.at[rows_of(s)], resid_h.at[rows_of(s)])
-
-    token_jobs[0].hop(2)
-    token_jobs[1].hop(1)
-    for step in range(3, tp // 2):
-        token_jobs[0].hop(step)
-        token_jobs[1].hop(step - 1)
-    wq_jobs[0].hop(1)
-    token_jobs[0].gathered()
-    sq_job.gathered()
-    wkv_job.gathered()
+            total = total + stat_all[t, s]
+        lane = lax.broadcasted_iota(jnp.int32, total.shape, 1)
+        logits = total * lax.rsqrt(total[7:8] / width + EPS)
+        return jnp.where(lane < lengths_s[s], logits, jnp.float32(0.0))
+
+    tok[1][0].begin()
+    sq.hop(1, DOWN)
+    tok[1][1].begin()
+    tok[0][1].hop(1, DOWN)
+    tok[0][0].turn()
+    tok[0][1].hop(1, UP)
+    sq.hop(1, UP)
+    sq.hop(2, DOWN)
+    tok[0][1].hop(2, DOWN)
+    tok[0][0].hop(1, UP)
+    tok[0][1].hop(2, UP)
+    tok[1][1].hop(1, UP)
+    tok[0][1].hop(3, UP)
+    judges()
+    wkv.arrive()
+    sq.hop(2, UP)
+    tok[1][1].hop(1, DOWN)
+    sq.hop(3, DOWN)
+    tok[0][1].hop(3, DOWN)
+    tok[0][0].hop(2, UP)
+    sq.hop(3, UP)
+    tok[0][0].hop(3, UP)
+    tok[0][0].hop(1, DOWN)
+    tok[0][0].hop(2, DOWN)
+    wq[0].arrive()
+    tok[1][1].hop(2, UP)
+    tok[1][1].hop(2, DOWN)
+    tok[1][0].turn()
+    tok[0][0].hop(3, DOWN)
     project_kv(0)
-    token_jobs[1].hop(tp // 2 - 1)
-    wq_jobs[0].gathered()
+    tok[1][1].hop(3, DOWN)
+    tok[1][1].hop(3, UP)
+    tok[1][0].hop(1, DOWN)
+    kv[0].hop(1, UP)
+    tok[1][0].hop(1, UP)
+    kv[0].hop(1, DOWN)
+    kv[0].hop(2, UP)
+    wq[1].arrive()
+    tok[1][0].hop(2, UP)
+    kv[0].hop(2, DOWN)
+    tok[1][0].hop(2, DOWN)
+    kv[0].hop(3, UP)
+    project_q(0, 1)
     project_q(0, 0)
-    for step in range(1, tp // 2):
-        kv_jobs[0].hop(step)
-    for j in range(1, q_steps):
-        wq_jobs[j].hop(1)
-        wq_jobs[j].gathered()
-        project_q(0, j)
-    kv_jobs[0].gathered()
-    attend(0)
-    token_jobs[1].gathered()
+    kv[0].hop(3, DOWN)
+    tok[1][0].hop(3, UP)
+    tok[1][0].hop(3, DOWN)
     project_kv(1)
-    att_jobs[0].turn()
-    kv_jobs[1].hop(1)
+    attend(0, 1)
+    attend(0, 0)
+    kv[1].hop(1, UP)
+    project_q(1, 1)
+    kv[1].hop(1, DOWN)
+    att[0][1][1].hop(1, DOWN)
+    kv[1].hop(2, DOWN)
+    att[0][1][0].turn()
+    kv[1].hop(3, DOWN)
+    kv[1].hop(2, UP)
+    att[0][0][1].hop(1, UP)
+    att[0][0][1].hop(1, DOWN)
     project_q(1, 0)
-    att_jobs[0].hop(1)
-    kv_jobs[1].hop(2)
-    for j in range(1, q_steps):
-        project_q(1, j)
-    for step in range(3, tp // 2):
-        kv_jobs[1].hop(step)
-    kv_jobs[1].gathered()
-    attend(1)
-    wo_jobs[0].hop(1)
-    att_jobs[1].turn()
-    att_jobs[0].hop(2)
-    wo_jobs[1].hop(1)
-    att_jobs[1].hop(1)
-    for step in range(3, tp // 2):
-        att_jobs[0].hop(step)
-        att_jobs[1].hop(step - 1)
-    att_jobs[0].gathered()
-    for n in range(2):
-        wo_jobs[n].gathered()
-        project_out(0, n)
-    att_jobs[1].hop(tp // 2 - 1)
-    for n in range(2, o_steps):
-        wo_jobs[n].hop(1)
-        wo_jobs[n].gathered()
-        project_out(0, n)
-    statistics(0)
-    writes = [write_out(0)]
-    att_jobs[1].gathered()
-    for n in range(o_steps):
-        project_out(1, n)
-    statistics(1)
-    writes.append(write_out(1))
-    conclude(0)
-    conclude(1)
-    last = fetch(score, score_h)
-    for job in token_jobs + att_jobs + kv_jobs + [wkv_job] + wq_jobs + wo_jobs + [sq_job] + stat_jobs:
+    kv[1].hop(3, UP)
+    att[0][1][1].hop(1, UP)
+    wo[0].arrive()
+    att[0][0][0].turn()
+    att[0][0][1].hop(2, UP)
+    att[0][1][1].hop(2, UP)
+    att[0][1][1].hop(2, DOWN)
+    att[0][1][0].hop(1, UP)
+    attend(1, 0)
+    attend(1, 1)
+    att[0][1][0].hop(2, UP)
+    att[0][1][1].hop(3, UP)
+    att[0][0][1].hop(2, DOWN)
+    wo[1].arrive()
+    att[0][0][1].hop(3, UP)
+    att[1][0][1].hop(1, DOWN)
+    att[1][0][1].hop(1, UP)
+    att[1][1][0].turn()
+    att[0][0][0].hop(1, UP)
+    att[0][1][0].hop(1, DOWN)
+    att[1][1][1].hop(1, UP)
+    att[1][0][1].hop(2, DOWN)
+    att[1][1][1].hop(1, DOWN)
+    att[1][0][1].hop(3, DOWN)
+    att[1][1][0].hop(1, DOWN)
+    att[1][1][1].hop(2, UP)
+    att[0][0][1].hop(3, DOWN)
+    att[0][0][0].hop(2, UP)
+    att[0][1][1].hop(3, DOWN)
+    att[0][1][0].hop(3, UP)
+    att[0][0][0].hop(1, DOWN)
+    att[1][0][0].turn()
+    att[1][0][1].hop(2, UP)
+    att[1][1][1].hop(2, DOWN)
+    att[0][0][0].hop(2, DOWN)
+    att[1][0][0].hop(1, UP)
+    att[1][1][0].hop(1, UP)
+    att[1][0][0].hop(1, DOWN)
+    att[1][1][0].hop(2, DOWN)
+    att[1][1][1].hop(3, UP)
+    wo[2].arrive()
+    att[0][0][0].hop(3, DOWN)
+    att[1][1][1].hop(3, DOWN)
+    att[1][0][1].hop(3, UP)
+    att[0][1][0].hop(2, DOWN)
+    att[0][0][0].hop(3, UP)
+    att[1][0][0].hop(2, UP)
+    att[1][1][0].hop(3, DOWN)
+    att[1][1][0].hop(2, UP)
+    att[0][1][0].hop(3, DOWN)
+    project_out(0)
+    att[1][0][0].hop(2, DOWN)
+    att[1][0][0].hop(3, UP)
+    wo[3].arrive()
+    att[1][1][0].hop(3, UP)
+    att[1][0][0].hop(3, DOWN)
+    project_out(1)
+    project_last()
+    stat.begin()
+    writes = [fetch(resid, resid_h)]
+    for job in sum(tok + sum(att, []), []) + kv + [sq, wkv] + wq + wo:
         job.drain()
+    stat.gathered()
+    lines = [conclude(s) for s in range(sequences)]
+    score[...] = jnp.concatenate(lines, axis=1)[: score.shape[0]]
+    writes.append(fetch(score, score_h))
+    stat.drain()
     for copy in writes:
         copy.wait()
-    last.wait()
+
+
+def pass_on_kernel(pieces, resid_in, score_in, resid_out, score_out, resid, score, sems):
+    rows = resid.shape[0] // pieces
+    parts = [slice(i * rows, (i + 1) * rows) for i in range(pieces)]
+    sources = [score_in] + [resid_in.at[p] for p in parts]
+    places = [score] + [resid.at[p] for p in parts]
+    targets = [score_out] + [resid_out.at[p] for p in parts]
+    into = [
+        pltpu.make_async_copy(a, b, sems.at[0, i]) for i, (a, b) in enumerate(zip(sources, places))
+    ]
+    out = [
+        pltpu.make_async_copy(a, b, sems.at[1, i]) for i, (a, b) in enumerate(zip(places, targets))
+    ]
+    for copy in into:
+        copy.start()
+    for first, second in zip(into, out):
+        first.wait()
+        second.start()
+    for copy in out:
+        copy.wait()
+
+
+def hand_over(resid, score):
+    pieces = 4
+    anywhere = pl.BlockSpec(memory_space=pl.ANY)
+    return pl.pallas_call(
+        functools.partial(pass_on_kernel, pieces),
+        out_shape=tuple(jax.ShapeDtypeStruct(a.shape, a.dtype) for a in (resid, score)),
+        in_specs=[anywhere] * 2,
+        out_specs=(anywhere,) * 2,
+        scratch_shapes=[
+            pltpu.VMEM(resid.shape, resid.dtype),
+            pltpu.VMEM(score.shape, score.dtype),
+            pltpu.SemaphoreType.DMA((2, pieces + 1)),
+        ],
+    )(resid, score)
 
 
 def whole_layer(
@@ -979,9 +1088,9 @@
         functools.partial(layer_kernel, sizes),
         out_shape=(
             jax.ShapeDtypeStruct((rows, features), half),
-            jax.ShapeDtypeStruct((sequences, 8, length), single),
+            jax.ShapeDtypeStruct((value_head.shape[1], rows), single),
         ),
-        in_specs=[pl.BlockSpec(memory_space=pltpu.SMEM)] + [anywhere] * 8,
+        in_specs=[pl.BlockSpec(memory_space=pltpu.SMEM)] + [pl.BlockSpec(memory_space=pltpu.HBM)] * 8,
         out_specs=(anywhere, anywhere),
         scratch_shapes=[
             vmem((tp, rows, features), half),
@@ -989,18 +1098,19 @@
             vmem((q_steps, rep, depth, STEP), half),
             vmem((o_steps, rep, mixed, STEP), half),
             vmem((sequences, tp, 2 * kv_cols, length), half),
-            vmem((tp, rows, head_cols), half),
+            vmem((q_steps, tp, rows, STEP), half),
             vmem((tp, 8, rows), single),
-            vmem((sequences, tp, 8, length), single),
+            vmem((tp, sequences, 8, length), single),
             vmem((rows, features), half),
             vmem((1, features), single),
             vmem((1, features), single),
             vmem((value_head.shape[1], features), single),
+            vmem((32, features), half),
             vmem((sequences, length, head_cols), half),
             vmem((rows, features), half),
-            vmem((sequences, 8, length), single),
+            vmem((value_head.shape[1], rows), single),
             dma((SEMAPHORES,)),
-            dma((32,)),
+            dma((16,)),
         ],
         compiler_params=pltpu.CompilerParams(
             collective_id=4, has_side_effects=True, vmem_limit_bytes=64 * 1024 * 1024 - 128 * 1024
@@ -1016,10 +1126,8 @@
         final_gain[None, :],
         value_head.T,
     )
-    position = jnp.arange(length, dtype=jnp.int32)
-    live = position[None, :] < row_lengths[:, None]
-    score = jnp.where(live[:, None, :], score[:, : value_head.shape[1]], jnp.float32(0.0))
-    return resid, score.transpose(0, 2, 1).reshape(rows, -1)
+    resid, score = hand_over(resid, score)
+    return resid, score.T
 
 
 def fits(sizes, tokens, row_lengths, query_weight, key_weight):
@@ -1028,11 +1136,11 @@
         row_lengths.shape[0] == 2
         and sizes["rep"] == 4
         and sizes["tp"] % sizes["rep"] == 0
-        and sizes["tp"] >= 8
+        and sizes["tp"] == 8
         and heads > 0
         and heads % KEY_VALUE_HEADS == 0
-        and query_weight.shape[1] % STEP == 0
-        and tokens.shape[1] % STEP == 0
+        and query_weight.shape[1] == 2 * STEP
+        and tokens.shape[1] == 4 * STEP
         and HEAD_SIZE % key_weight.shape[1] == 0
     )
 

time: 139 us -> 124 us (0.89)
  Pallas kernels: 135 us -> 123 us
  local copies, waits for them, and re-layouts: 2.76 us -> 0 us
    pallas_call x1, Pallas kernels: 135 us -> 121 us  [whole_layer(): pl.pallas_call(functools.partial(layer_kernel, sizes), out_shape=(jax.Sha...]
    unnamed x3 -> x0, local copies, waits for them, and re-layouts: 2.07 us -> none
    pallas_call x0 -> x1, Pallas kernels: none -> 2 us  [hand_over(): pl.pallas_call(functools.partial(pass_on_kernel, pieces), out_shape=tuple...]
where the time goes in v2:
time: 124 us
  Pallas kernels  123 us (99%)
    pallas_call x1, Pallas kernels, whole_layer(): pl.pallas_call(functools.partial(layer_kernel, sizes), out_shape=(jax.Sha...  121 us

profile of v2, /device:TPU:0, one launch (start us, length us, event | category | flops | bytes accessed | tf_op | source)
XLA Modules:
  0.0 123.9 jit_solution(12191071885312924442)
XLA Ops:
  0.6 121.3 %shard_map.104 = (bf16[384,1024]{1,0:T(8,128)(2,1)}, f32[6,384]{1,0:T(8,128)}) custom-call(s32[2]{0:T(128)} %lengths_s.1, bf16[384,1024]{1,0:T(8,128)(2,1)} %tokens_h.1, f32[1,1024]{1,0:T(1,128)} %bitcast.9, bf16[2048,512]{1,0:T(8,128)(2,1)} %query_h.1, bf16[64,2048]{1,0:T(8,128)(2,1)} %bitcast.6, bf16[64,2048]{1,0:T(8,128)(2,1)} %bitcast.7, ...), custom_call_target="tpu_custom_call" | custom-call | tf_op jit(solution)/shard_map/pallas_call | solution.py:1087
  121.9 2.0 %shard_map.105 = (bf16[384,1024]{1,0:T(8,128)(2,1)}, f32[6,384]{1,0:T(8,128)}) custom-call(bf16[384,1024]{1,0:T(8,128)(2,1)} %get-tuple-element.6.resid_in, f32[6,384]{1,0:T(8,128)} %get-tuple-element.7.score_in), custom_call_target="tpu_custom_call" | custom-call | tf_op jit(solution)/shard_map/pallas_call | solution.py:1051

commit v3 on v2

--- a/solution.py
+++ b/solution.py
@@ -695,6 +695,7 @@
     att_all,
     sq_all,
     stat_all,
+    stat_here,
     raw,
     gain,
     fgain,
@@ -864,7 +865,7 @@
         sums = sums[0:8] + sums[8:16] + sums[16:24]
         line = lax.broadcasted_iota(jnp.int32, sums.shape, 0)
         sums = jnp.where(line == 7, row_sums_of_squares(block), sums)
-        stat_all[me_t, s] += sums
+        stat_here[s] += sums
         return 0
 
     def project_out(s):
@@ -881,143 +882,144 @@
         rest = jnp.zeros((8 - heads.shape[0], features), jnp.float32)
         weight = jnp.concatenate([weight, rest], axis=0)
         parts = [p.astype(jnp.float32) for p in exact_parts(weight, 3)]
-        stat_all[me_t] = jnp.zeros(stat_all.shape[1:], jnp.float32)
+        stat_here[...] = jnp.zeros_like(stat_here)
         judge[...] = jnp.concatenate(parts + [jnp.zeros_like(weight)], axis=0).astype(jnp.bfloat16)
 
-    def conclude(s):
-        total = stat_all[0, s]
+    def conclude():
+        total = stat_all[0]
         for t in range(1, tp):
-            total = total + stat_all[t, s]
-        lane = lax.broadcasted_iota(jnp.int32, total.shape, 1)
+            total = total + stat_all[t]
+        position = lax.broadcasted_iota(jnp.int32, (total.shape[0], length), 1)
+        live = [(position < lengths_s[s]).astype(jnp.float32) for s in range(sequences)]
         logits = total * lax.rsqrt(total[7:8] / width + EPS)
-        return jnp.where(lane < lengths_s[s], logits, jnp.float32(0.0))
-
+        return jnp.where(jnp.concatenate(live, axis=1) > 0.5, logits, jnp.float32(0.0))
+
+    sq.hop(1, DOWN)
+    sq.hop(1, UP)
+    tok[1][1].begin()
+    tok[0][1].hop(1, UP)
+    sq.hop(2, DOWN)
+    tok[0][1].hop(1, DOWN)
+    tok[1][1].hop(1, DOWN)
+    tok[0][1].hop(2, DOWN)
+    sq.hop(2, UP)
     tok[1][0].begin()
-    sq.hop(1, DOWN)
-    tok[1][1].begin()
-    tok[0][1].hop(1, DOWN)
     tok[0][0].turn()
-    tok[0][1].hop(1, UP)
-    sq.hop(1, UP)
-    sq.hop(2, DOWN)
-    tok[0][1].hop(2, DOWN)
+    tok[0][1].hop(2, UP)
     tok[0][0].hop(1, UP)
-    tok[0][1].hop(2, UP)
+    tok[0][1].hop(3, DOWN)
     tok[1][1].hop(1, UP)
+    tok[0][0].hop(1, DOWN)
     tok[0][1].hop(3, UP)
+    tok[0][0].hop(2, UP)
+    wq[0].arrive()
+    sq.hop(3, DOWN)
+    sq.hop(3, UP)
+    tok[0][0].hop(3, UP)
+    tok[0][0].hop(2, DOWN)
+    tok[1][1].hop(2, DOWN)
+    tok[0][0].hop(3, DOWN)
+    tok[1][1].hop(2, UP)
     judges()
     wkv.arrive()
-    sq.hop(2, UP)
-    tok[1][1].hop(1, DOWN)
-    sq.hop(3, DOWN)
-    tok[0][1].hop(3, DOWN)
-    tok[0][0].hop(2, UP)
-    sq.hop(3, UP)
-    tok[0][0].hop(3, UP)
-    tok[0][0].hop(1, DOWN)
-    tok[0][0].hop(2, DOWN)
-    wq[0].arrive()
-    tok[1][1].hop(2, UP)
-    tok[1][1].hop(2, DOWN)
     tok[1][0].turn()
-    tok[0][0].hop(3, DOWN)
     project_kv(0)
     tok[1][1].hop(3, DOWN)
     tok[1][1].hop(3, UP)
+    tok[1][0].hop(1, UP)
+    kv[0].hop(1, UP)
+    kv[0].hop(1, DOWN)
+    project_q(0, 0)
     tok[1][0].hop(1, DOWN)
-    kv[0].hop(1, UP)
-    tok[1][0].hop(1, UP)
-    kv[0].hop(1, DOWN)
+    wq[1].arrive()
     kv[0].hop(2, UP)
-    wq[1].arrive()
     tok[1][0].hop(2, UP)
     kv[0].hop(2, DOWN)
     tok[1][0].hop(2, DOWN)
+    kv[0].hop(3, DOWN)
     kv[0].hop(3, UP)
     project_q(0, 1)
-    project_q(0, 0)
-    kv[0].hop(3, DOWN)
     tok[1][0].hop(3, UP)
     tok[1][0].hop(3, DOWN)
     project_kv(1)
     attend(0, 1)
     attend(0, 0)
+    kv[1].hop(1, DOWN)
     kv[1].hop(1, UP)
-    project_q(1, 1)
-    kv[1].hop(1, DOWN)
+    project_q(1, 0)
+    att[0][1][0].turn()
+    att[0][1][1].hop(1, UP)
+    kv[1].hop(2, UP)
+    att[0][0][0].turn()
     att[0][1][1].hop(1, DOWN)
     kv[1].hop(2, DOWN)
-    att[0][1][0].turn()
+    att[0][0][1].hop(1, UP)
+    kv[1].hop(3, UP)
+    att[0][0][1].hop(1, DOWN)
+    project_q(1, 1)
     kv[1].hop(3, DOWN)
-    kv[1].hop(2, UP)
-    att[0][0][1].hop(1, UP)
-    att[0][0][1].hop(1, DOWN)
-    project_q(1, 0)
-    kv[1].hop(3, UP)
-    att[0][1][1].hop(1, UP)
+    att[0][1][1].hop(2, DOWN)
+    att[0][1][1].hop(2, UP)
+    att[0][0][1].hop(2, UP)
+    att[0][0][1].hop(2, DOWN)
+    attend(1, 1)
+    att[0][1][0].hop(1, DOWN)
+    att[0][0][0].hop(1, UP)
+    att[0][1][0].hop(1, UP)
+    att[0][1][1].hop(3, DOWN)
+    attend(1, 0)
+    att[1][1][1].hop(1, DOWN)
+    att[1][1][1].hop(1, UP)
+    att[1][1][0].turn()
+    att[1][0][1].hop(1, DOWN)
     wo[0].arrive()
-    att[0][0][0].turn()
-    att[0][0][1].hop(2, UP)
-    att[0][1][1].hop(2, UP)
-    att[0][1][1].hop(2, DOWN)
-    att[0][1][0].hop(1, UP)
-    attend(1, 0)
-    attend(1, 1)
     att[0][1][0].hop(2, UP)
+    att[1][0][1].hop(1, UP)
+    att[1][1][1].hop(2, UP)
+    att[1][0][0].turn()
+    att[0][0][0].hop(2, UP)
     att[0][1][1].hop(3, UP)
-    att[0][0][1].hop(2, DOWN)
+    att[1][1][1].hop(2, DOWN)
+    att[1][0][1].hop(2, UP)
+    att[0][0][0].hop(1, DOWN)
+    att[1][0][1].hop(2, DOWN)
+    att[0][0][1].hop(3, UP)
+    att[1][0][0].hop(1, DOWN)
     wo[1].arrive()
-    att[0][0][1].hop(3, UP)
-    att[1][0][1].hop(1, DOWN)
-    att[1][0][1].hop(1, UP)
-    att[1][1][0].turn()
-    att[0][0][0].hop(1, UP)
-    att[0][1][0].hop(1, DOWN)
-    att[1][1][1].hop(1, UP)
-    att[1][0][1].hop(2, DOWN)
-    att[1][1][1].hop(1, DOWN)
+    att[0][1][0].hop(2, DOWN)
+    wo[2].arrive()
+    att[1][1][0].hop(1, UP)
+    att[0][0][1].hop(3, DOWN)
+    att[1][1][1].hop(3, UP)
+    att[1][1][0].hop(1, DOWN)
+    att[1][0][0].hop(1, UP)
+    att[1][1][1].hop(3, DOWN)
+    att[0][0][0].hop(3, UP)
+    att[1][0][1].hop(3, UP)
+    att[0][1][0].hop(3, UP)
     att[1][0][1].hop(3, DOWN)
-    att[1][1][0].hop(1, DOWN)
-    att[1][1][1].hop(2, UP)
-    att[0][0][1].hop(3, DOWN)
-    att[0][0][0].hop(2, UP)
-    att[0][1][1].hop(3, DOWN)
-    att[0][1][0].hop(3, UP)
-    att[0][0][0].hop(1, DOWN)
-    att[1][0][0].turn()
-    att[1][0][1].hop(2, UP)
-    att[1][1][1].hop(2, DOWN)
     att[0][0][0].hop(2, DOWN)
-    att[1][0][0].hop(1, UP)
-    att[1][1][0].hop(1, UP)
-    att[1][0][0].hop(1, DOWN)
     att[1][1][0].hop(2, DOWN)
-    att[1][1][1].hop(3, UP)
-    wo[2].arrive()
+    att[1][0][0].hop(2, UP)
     att[0][0][0].hop(3, DOWN)
-    att[1][1][1].hop(3, DOWN)
-    att[1][0][1].hop(3, UP)
-    att[0][1][0].hop(2, DOWN)
-    att[0][0][0].hop(3, UP)
-    att[1][0][0].hop(2, UP)
-    att[1][1][0].hop(3, DOWN)
     att[1][1][0].hop(2, UP)
+    att[1][0][0].hop(3, UP)
     att[0][1][0].hop(3, DOWN)
     project_out(0)
+    att[1][1][0].hop(3, UP)
+    att[1][1][0].hop(3, DOWN)
     att[1][0][0].hop(2, DOWN)
-    att[1][0][0].hop(3, UP)
+    att[1][0][0].hop(3, DOWN)
     wo[3].arrive()
-    att[1][1][0].hop(3, UP)
-    att[1][0][0].hop(3, DOWN)
     project_out(1)
     project_last()
+    stat_all[me_t] = jnp.concatenate([stat_here[s] for s in range(sequences)], axis=1)
     stat.begin()
     writes = [fetch(resid, resid_h)]
     for job in sum(tok + sum(att, []), []) + kv + [sq, wkv] + wq + wo:
         job.drain()
     stat.gathered()
-    lines = [conclude(s) for s in range(sequences)]
-    score[...] = jnp.concatenate(lines, axis=1)[: score.shape[0]]
+    score[...] = conclude()[: score.shape[0]]
     writes.append(fetch(score, score_h))
     stat.drain()
     for copy in writes:
@@ -1100,7 +1102,8 @@
             vmem((sequences, tp, 2 * kv_cols, length), half),
             vmem((q_steps, tp, rows, STEP), half),
             vmem((tp, 8, rows), single),
-            vmem((tp, sequences, 8, length), single),
+            vmem((tp, 8, rows), single),
+            vmem((sequences, 8, length), single),
             vmem((rows, features), half),
             vmem((1, features), single),
             vmem((1, features), single),

time: 124 us -> 124 us (level)
  no operation moved by 1% of the time
where the time goes in v3:
time: 124 us
  Pallas kernels  123 us (99%)
    pallas_call x1, Pallas kernels, whole_layer(): pl.pallas_call(functools.partial(layer_kernel, sizes), out_shape=(jax.Sha...  121 us

profile of v3, /device:TPU:0, one launch (start us, length us, event | category | flops | bytes accessed | tf_op | source)
XLA Modules:
  0.0 123.7 jit_solution(13197501999148056964)
XLA Ops:
  0.6 121.0 %shard_map.104 = (bf16[384,1024]{1,0:T(8,128)(2,1)}, f32[6,384]{1,0:T(8,128)}) custom-call(s32[2]{0:T(128)} %lengths_s.1, bf16[384,1024]{1,0:T(8,128)(2,1)} %tokens_h.1, f32[1,1024]{1,0:T(1,128)} %bitcast.9, bf16[2048,512]{1,0:T(8,128)(2,1)} %query_h.1, bf16[64,2048]{1,0:T(8,128)(2,1)} %bitcast.6, bf16[64,2048]{1,0:T(8,128)(2,1)} %bitcast.7, ...), custom_call_target="tpu_custom_call" | custom-call | tf_op jit(solution)/shard_map/pallas_call | solution.py:1089
  121.7 2.0 %shard_map.105 = (bf16[384,1024]{1,0:T(8,128)(2,1)}, f32[6,384]{1,0:T(8,128)}) custom-call(bf16[384,1024]{1,0:T(8,128)(2,1)} %get-tuple-element.6.resid_in, f32[6,384]{1,0:T(8,128)} %get-tuple-element.7.score_in), custom_call_target="tpu_custom_call" | custom-call | tf_op jit(solution)/shard_map/pallas_call | solution.py:1053
